TPU v7x, 32 devices: a whole 2x2x4 slice. The times are simulated.
32 devices in a mesh: fsdp: 4 (over z), ctx: 4 (over x, core), tp: 2 (over y).
Axes of the slice: x: 2, y: 2, z: 4, core: 2. Of those that a mesh axis runs over, the one named last changes fastest.
Arguments:
- layer_input: float32 [4, 4096, 512], P('fsdp', 'ctx'), may hold values from -6 to 6
- out_grad: float32 [4, 4096, 512], P('fsdp', 'ctx'), may hold values from -6 to 6
- lengths: int32 [4], P('fsdp'), may hold values from 1024 to 4096, as said below
- norm_gains: float32 [5, 512], replicated, may hold values from 0.5 to 1.5
- feed_up: bfloat16 [512, 2048], P('fsdp', 'tp'), may hold values from -0.25 to 0.25
- feed_down: bfloat16 [512, 2048], P('fsdp', 'tp'), may hold values from -0.125 to 0.125
- attend_in: bfloat16 [512, 3, 512], P('fsdp', None, 'tp'), may hold values from -0.25 to 0.25
- attend_out: bfloat16 [512, 512], P('fsdp', 'tp'), may hold values from -6 to 6
- mixer_in: bfloat16 [512, 2, 512], P('fsdp', None, 'tp'), may hold values from -0.25 to 0.25
- mixer_out: bfloat16 [512, 512], P('fsdp', 'tp'), may hold values from -0.25 to 0.25
- depth_kernel: float32 [31, 512], P(None, 'tp'), may hold values from -1.5 to 1.5
- batch_norm: float32 [2, 512], P(None, 'tp'), may hold values from 0.5 to 1.5
- final_up: bfloat16 [512, 2048], P('fsdp', 'tp'), may hold values from -0.25 to 0.25
- final_down: bfloat16 [512, 2048], P('fsdp', 'tp'), may hold values from -0.125 to 0.125
Outputs:
- layer_output: float32 [4, 4096, 512], P('fsdp', 'ctx')
- input_grad: float32 [4, 4096, 512], P('fsdp', 'ctx')
- gains_grad: float32 [5, 512], replicated
- feed_up_grad: float32 [512, 2048], P('fsdp', 'tp')
- feed_down_grad: float32 [512, 2048], P('fsdp', 'tp')
- attend_in_grad: float32 [512, 3, 512], P('fsdp', None, 'tp')
- attend_out_grad: float32 [512, 512], P('fsdp', 'tp')
- mixer_in_grad: float32 [512, 2, 512], P('fsdp', None, 'tp')
- mixer_out_grad: float32 [512, 512], P('fsdp', 'tp')
- kernel_grad: float32 [31, 512], P(None, 'tp')
- norm_grad: float32 [2, 512], P(None, 'tp')
- final_up_grad: float32 [512, 2048], P('fsdp', 'tp')
- final_down_grad: float32 [512, 2048], P('fsdp', 'tp')
Inputs may be any that keep to these rules, and one draw needn't show every extreme that they name: `lengths`: every utterance has at least a quarter of its 4096 frames, and one of them has all 4096.
All inputs are finite; a program needn't handle non-finite values.
Results may differ from a plain program's by a relative error of at most 0.038.
Values may be sent and summed in bfloat16 or wider, within the bound.
A program may use at most 384 MiB of HBM per device.

v0:
```python
import jax
import jax.numpy as jnp
from jax import lax
from jax.sharding import PartitionSpec as P

HEAD = 64
KERNEL = 31
norm_eps = 1e-05
masked_score = -1000000000.0


def with_halo(cells, sides, width):
    for axis, dim in sides:
        count = lax.axis_size(axis)
        ends = count - 1
        head = lax.slice_in_dim(cells, 0, width, axis=dim)
        tail = lax.slice_in_dim(cells, cells.shape[dim] - width, cells.shape[dim], axis=dim)
        cells = jnp.concatenate(
            [
                lax.ppermute(tail, axis, [(i, (i + 1) % count) for i in range(ends)]),
                cells,
                lax.ppermute(head, axis, [((i + 1) % count, i) for i in range(ends)]),
            ],
            axis=dim,
        )
    return cells


def layer_norm(values, gain):
    center = values - jnp.mean(values, -1, keepdims=True)
    spread = jnp.mean(center * center, -1, keepdims=True)
    return center * lax.rsqrt(spread + norm_eps) * gain


def rotary(values, position):
    half = values.shape[-1] // 2
    inverse = 10000.0 ** (-2.0 * jnp.arange(half, dtype=jnp.float32) / values.shape[-1])
    angle = position.astype(jnp.float32)[:, None] * inverse[None, :]
    cosine = jnp.cos(angle)[:, None, :]
    sine = jnp.sin(angle)[:, None, :]
    lower = values[..., :half]
    upper = values[..., half:]
    return jnp.concatenate([lower * cosine - upper * sine, lower * sine + upper * cosine], -1)


def swish(values):
    return values * jax.nn.sigmoid(values)


def tensor_total(partial_value):
    return lax.psum(partial_value.astype(jnp.bfloat16), "tp").astype(jnp.float32)


def product_rows(left, right):
    return lax.dot_general(
        left, right, (((1,), (1,)), ((), ())), preferred_element_type=jnp.float32
    )


def product_cols(left, right):
    return lax.dot_general(
        left, right, (((0,), (0,)), ((), ())), preferred_element_type=jnp.float32
    )


def feed_forward(stream, gain, weight_up, weight_down):
    normed, norm_back = jax.vjp(layer_norm, stream, gain)
    normed_low = normed.astype(jnp.bfloat16)
    hidden = jnp.dot(normed_low, weight_up, preferred_element_type=jnp.float32)
    active, active_back = jax.vjp(swish, hidden)
    active_low = active.astype(jnp.bfloat16)
    branch = tensor_total(product_rows(active_low, weight_down))
    return (branch, (norm_back, normed_low, active_back, active_low))


def feed_backward(branch_grad, saved, weight_up, weight_down):
    norm_back, normed_low, active_back, active_low = saved
    grad_low = branch_grad.astype(jnp.bfloat16)
    down_grad = product_cols(grad_low, active_low)
    hidden_grad = active_back(jnp.dot(grad_low, weight_down, preferred_element_type=jnp.float32))[
        0
    ].astype(jnp.bfloat16)
    up_grad = product_cols(normed_low, hidden_grad)
    normed_grad = tensor_total(product_rows(hidden_grad, weight_up))
    stream_grad, gain_grad = norm_back(normed_grad)
    return (stream_grad, gain_grad, up_grad, down_grad)


def split_joined(joined, heads):
    width = heads * HEAD
    keys = joined[:, :width].reshape(joined.shape[0], heads, HEAD)
    values = joined[:, width:].reshape(joined.shape[0], heads, HEAD)
    return (keys, values)


def attend_scores(query, keys, length):
    scores = jnp.einsum("fhe,lhe->hfl", query, keys, preferred_element_type=jnp.float32)
    live_keys = jnp.arange(keys.shape[0]) < length
    return jnp.where(live_keys[None, None, :], scores, masked_score)


def attend_one(inputs):
    query, joined, length = inputs
    keys, values = split_joined(joined, query.shape[1])
    scores = attend_scores(query, keys, length)
    top = jnp.max(scores, -1, keepdims=True)
    raised = jnp.exp(scores - top)
    total = jnp.sum(raised, -1, keepdims=True)
    weights = (raised / total).astype(jnp.bfloat16)
    mixed = jnp.einsum("hfl,lhe->fhe", weights, values, preferred_element_type=jnp.float32)
    return (mixed.astype(jnp.bfloat16), (top + jnp.log(total))[..., 0])


def attend_back(inputs):
    query, joined, length, log_total, mixed_grad = inputs
    keys, values = split_joined(joined, query.shape[1])
    scores = attend_scores(query, keys, length)
    probs = jnp.exp(scores - log_total[..., None])
    probs_grad = jnp.einsum("fhe,lhe->hfl", mixed_grad, values, preferred_element_type=jnp.float32)
    center = jnp.sum(probs * probs_grad, -1, keepdims=True)
    score_grad = (probs * (probs_grad - center)).astype(jnp.bfloat16)
    query_grad = jnp.einsum("hfl,lhe->fhe", score_grad, keys, preferred_element_type=jnp.float32)
    keys_grad = jnp.einsum("hfl,fhe->lhe", score_grad, query, preferred_element_type=jnp.float32)
    values_grad = jnp.einsum(
        "hfl,fhe->lhe", probs.astype(jnp.bfloat16), mixed_grad, preferred_element_type=jnp.float32
    )
    frames_all = keys.shape[0]
    joined_grad = jnp.concatenate(
        [keys_grad.reshape(frames_all, -1), values_grad.reshape(frames_all, -1)], -1
    )
    return (query_grad, joined_grad)


def per_device(
    layer_input,
    out_grad,
    lengths,
    norm_gains,
    feed_up,
    feed_down,
    attend_in,
    attend_out,
    mixer_in,
    mixer_out,
    depth_kernel,
    batch_norm,
    final_up,
    final_down,
):
    batch, frames, width = layer_input.shape
    rows = batch * frames
    place = lax.axis_index("ctx") * frames + jnp.arange(frames, dtype=jnp.int32)
    live = (place[None, :] < lengths[:, None]).astype(jnp.float32)
    live_rows = live.reshape(rows, 1)
    live_cube = live[:, :, None]
    gathered = (
        lax.all_gather(feed_up, "fsdp", axis=0, tiled=True),
        lax.all_gather(feed_down, "fsdp", axis=0, tiled=True),
        lax.all_gather(attend_in, "fsdp", axis=0, tiled=True),
        lax.all_gather(attend_out, "fsdp", axis=0, tiled=True),
        lax.all_gather(mixer_in, "fsdp", axis=0, tiled=True),
        lax.all_gather(mixer_out, "fsdp", axis=0, tiled=True),
        lax.all_gather(final_up, "fsdp", axis=0, tiled=True),
        lax.all_gather(final_down, "fsdp", axis=0, tiled=True),
    )
    up_one, down_one, proj_in, proj_out, conv_in, conv_out, up_two, down_two = gathered
    stream = layer_input.reshape(rows, width)
    cotangent = out_grad.reshape(rows, width)
    branch_one, saved_one = feed_forward(stream, norm_gains[0], up_one, down_one)
    after_one = stream + 0.5 * branch_one
    normed, norm_back_two = jax.vjp(layer_norm, after_one, norm_gains[1])
    normed_two = normed.astype(jnp.bfloat16)
    projected = jnp.einsum("nd,dke->nke", normed_two, proj_in, preferred_element_type=jnp.float32)
    local_width = projected.shape[2]
    heads = local_width // HEAD
    split = projected.reshape(batch, frames, 3, heads, HEAD)

    def rotate_pair(query_raw, key_raw):
        return (rotary(query_raw, place) * HEAD ** (-0.5), rotary(key_raw, place))

    (query_rot, key_rot), rotate_back = jax.vjp(rotate_pair, split[:, :, 0], split[:, :, 1])
    query_low = query_rot.astype(jnp.bfloat16)
    joined = jnp.concatenate(
        [
            key_rot.astype(jnp.bfloat16).reshape(batch, frames, local_width),
            split[:, :, 2].astype(jnp.bfloat16).reshape(batch, frames, local_width),
        ],
        -1,
    )
    joined_all = lax.all_gather(joined, "ctx", axis=1, tiled=True)
    mixed, log_total = lax.map(attend_one, (query_low, joined_all, lengths))
    mixed_rows = mixed.reshape(rows, local_width)
    after_two = after_one + tensor_total(product_rows(mixed_rows, proj_out))
    normed, norm_back_three = jax.vjp(layer_norm, after_two, norm_gains[2])
    normed_three = normed.astype(jnp.bfloat16)
    gates = jnp.einsum("nd,dke->nke", normed_three, conv_in, preferred_element_type=jnp.float32)

    def gate_linear(values):
        return values[:, 0] * jax.nn.sigmoid(values[:, 1]) * live_rows

    gated, gate_back = jax.vjp(gate_linear, gates)
    channels = gated.shape[1]
    gated_low = gated.astype(jnp.bfloat16).reshape(batch, frames, channels)
    reach = KERNEL // 2
    padded = with_halo(gated_low, (("ctx", 1),), reach)
    filtered = jnp.zeros((batch, frames, channels), jnp.float32)
    for offset in range(KERNEL):
        filtered = filtered + depth_kernel[offset] * padded[:, offset : offset + frames].astype(
            jnp.float32
        )
    sums = lax.psum(
        (
            jnp.sum(live_cube * filtered, (0, 1)),
            jnp.sum(live_cube * filtered * filtered, (0, 1)),
            jnp.sum(live),
        ),
        ("fsdp", "ctx"),
    )
    count = sums[2]
    mean = sums[0] / count
    variance = sums[1] / count - mean * mean
    rescale = lax.rsqrt(variance + norm_eps)
    unit = (filtered - mean) * rescale
    shifted = unit * batch_norm[0] + batch_norm[1]
    active, active_back = jax.vjp(swish, shifted.reshape(rows, channels))
    active_low = active.astype(jnp.bfloat16)
    after_three = after_two + tensor_total(product_rows(active_low, conv_out))
    branch_four, saved_four = feed_forward(after_three, norm_gains[3], up_two, down_two)
    after_four = after_three + 0.5 * branch_four
    result, final_back = jax.vjp(layer_norm, after_four, norm_gains[4])
    grad_four, gain_five = final_back(cotangent)
    stream_grad, gain_four, up_two_grad, down_two_grad = feed_backward(
        0.5 * grad_four, saved_four, up_two, down_two
    )
    grad_three = grad_four + stream_grad
    branch_low = grad_three.astype(jnp.bfloat16)
    conv_out_grad = product_cols(branch_low, active_low)
    shifted_grad = active_back(jnp.dot(branch_low, conv_out, preferred_element_type=jnp.float32))[
        0
    ].reshape(batch, frames, channels)
    bias_sum, scale_sum = lax.psum(
        (jnp.sum(shifted_grad, (0, 1)), jnp.sum(shifted_grad * unit, (0, 1))), ("fsdp", "ctx")
    )
    var_grad = -0.5 * rescale * rescale * batch_norm[0] * scale_sum
    first_grad = (-rescale * batch_norm[0] * bias_sum - 2.0 * mean * var_grad) / count
    second_grad = var_grad / count
    filtered_grad = (
        rescale * batch_norm[0] * shifted_grad
        + live_cube * (first_grad + 2.0 * filtered * second_grad)
    ).astype(jnp.bfloat16)
    padded_grad = with_halo(filtered_grad, (("ctx", 1),), reach)
    filtered_wide = filtered_grad.astype(jnp.float32)
    gated_grad = jnp.zeros((batch, frames, channels), jnp.float32)
    kernel_terms = []
    for offset in range(KERNEL):
        start = 2 * reach - offset
        gated_grad = gated_grad + depth_kernel[offset] * padded_grad[
            :, start : start + frames
        ].astype(jnp.float32)
        kernel_terms.append(
            jnp.sum(filtered_wide * padded[:, offset : offset + frames].astype(jnp.float32), (0, 1))
        )
    kernel_local = jnp.stack(kernel_terms)
    gates_grad = gate_back(gated_grad.reshape(rows, channels))[0].astype(jnp.bfloat16)
    conv_in_grad = jnp.einsum(
        "nd,nke->dke", normed_three, gates_grad, preferred_element_type=jnp.float32
    )
    normed_grad = tensor_total(
        jnp.einsum("nke,dke->nd", gates_grad, conv_in, preferred_element_type=jnp.float32)
    )
    stream_grad, gain_three = norm_back_three(normed_grad)
    grad_two = grad_three + stream_grad
    branch_low = grad_two.astype(jnp.bfloat16)
    proj_out_grad = product_cols(branch_low, mixed_rows)
    mixed_grad = (
        jnp.dot(branch_low, proj_out, preferred_element_type=jnp.float32)
        .astype(jnp.bfloat16)
        .reshape(batch, frames, heads, HEAD)
    )
    query_grad, joined_grad = lax.map(
        attend_back, (query_low, joined_all, lengths, log_total, mixed_grad)
    )
    joined_local = lax.psum_scatter(
        joined_grad.astype(jnp.bfloat16), "ctx", scatter_dimension=1, tiled=True
    ).astype(jnp.float32)
    key_grad = joined_local[..., :local_width].reshape(batch, frames, heads, HEAD)
    value_grad = joined_local[..., local_width:].reshape(batch, frames, heads, HEAD)
    query_raw_grad, key_raw_grad = rotate_back((query_grad, key_grad))
    proj_grad = (
        jnp.stack([query_raw_grad, key_raw_grad, value_grad], 2)
        .reshape(rows, 3, local_width)
        .astype(jnp.bfloat16)
    )
    proj_in_grad = jnp.einsum(
        "nd,nke->dke", normed_two, proj_grad, preferred_element_type=jnp.float32
    )
    normed_grad = tensor_total(
        jnp.einsum("nke,dke->nd", proj_grad, proj_in, preferred_element_type=jnp.float32)
    )
    stream_grad, gain_two = norm_back_two(normed_grad)
    grad_one = grad_two + stream_grad
    stream_grad, gain_one, up_one_grad, down_one_grad = feed_backward(
        0.5 * grad_one, saved_one, up_one, down_one
    )
    input_grad = grad_one + stream_grad
    gain_terms = jnp.stack([gain_one, gain_two, gain_three, gain_four, gain_five])
    gain_total, kernel_total = lax.psum((gain_terms, kernel_local), ("fsdp", "ctx"))
    weight_grads = (
        up_one_grad,
        down_one_grad,
        proj_in_grad,
        proj_out_grad,
        conv_in_grad,
        conv_out_grad,
        up_two_grad,
        down_two_grad,
    )
    owned = (
        lax.psum_scatter(
            weight_grads[0].astype(jnp.bfloat16), "fsdp", scatter_dimension=0, tiled=True
        ).astype(jnp.float32),
        lax.psum_scatter(
            weight_grads[1].astype(jnp.bfloat16), "fsdp", scatter_dimension=0, tiled=True
        ).astype(jnp.float32),
        lax.psum_scatter(
            weight_grads[2].astype(jnp.bfloat16), "fsdp", scatter_dimension=0, tiled=True
        ).astype(jnp.float32),
        lax.psum_scatter(
            weight_grads[3].astype(jnp.bfloat16), "fsdp", scatter_dimension=0, tiled=True
        ).astype(jnp.float32),
        lax.psum_scatter(
            weight_grads[4].astype(jnp.bfloat16), "fsdp", scatter_dimension=0, tiled=True
        ).astype(jnp.float32),
        lax.psum_scatter(
            weight_grads[5].astype(jnp.bfloat16), "fsdp", scatter_dimension=0, tiled=True
        ).astype(jnp.float32),
        lax.psum_scatter(
            weight_grads[6].astype(jnp.bfloat16), "fsdp", scatter_dimension=0, tiled=True
        ).astype(jnp.float32),
        lax.psum_scatter(
            weight_grads[7].astype(jnp.bfloat16), "fsdp", scatter_dimension=0, tiled=True
        ).astype(jnp.float32),
    )
    owned = (
        lax.psum(owned[0].astype(jnp.bfloat16), "ctx").astype(jnp.float32),
        lax.psum(owned[1].astype(jnp.bfloat16), "ctx").astype(jnp.float32),
        lax.psum(owned[2].astype(jnp.bfloat16), "ctx").astype(jnp.float32),
        lax.psum(owned[3].astype(jnp.bfloat16), "ctx").astype(jnp.float32),
        lax.psum(owned[4].astype(jnp.bfloat16), "ctx").astype(jnp.float32),
        lax.psum(owned[5].astype(jnp.bfloat16), "ctx").astype(jnp.float32),
        lax.psum(owned[6].astype(jnp.bfloat16), "ctx").astype(jnp.float32),
        lax.psum(owned[7].astype(jnp.bfloat16), "ctx").astype(jnp.float32),
    )
    return (
        result.reshape(batch, frames, width),
        input_grad.reshape(batch, frames, width),
        gain_total,
        owned[0],
        owned[1],
        owned[2],
        owned[3],
        owned[4],
        owned[5],
        kernel_total,
        jnp.stack([scale_sum, bias_sum]),
        owned[6],
        owned[7],
    )


def solution(mesh):
    placed = (
        P("fsdp", "ctx", None),
        P("fsdp", "ctx", None),
        P("fsdp"),
        P(),
        P("fsdp", "tp"),
        P("fsdp", "tp"),
        P("fsdp", None, "tp"),
        P("fsdp", "tp"),
        P("fsdp", None, "tp"),
        P("fsdp", "tp"),
        P(None, "tp"),
        P(None, "tp"),
        P("fsdp", "tp"),
        P("fsdp", "tp"),
    )
    return jax.shard_map(
        per_device,
        mesh=mesh,
        in_specs=placed,
        out_specs=(
            P("fsdp", "ctx", None),
            P("fsdp", "ctx", None),
            P(),
            P("fsdp", "tp"),
            P("fsdp", "tp"),
            P("fsdp", None, "tp"),
            P("fsdp", "tp"),
            P("fsdp", None, "tp"),
            P("fsdp", "tp"),
            P(None, "tp"),
            P(None, "tp"),
            P("fsdp", "tp"),
            P("fsdp", "tp"),
        ),
        check_vma=False,
    )
```

profile of v0, /device:TPU:0, one launch (start us, length us, event | category | flops | bytes accessed | tf_op | source)
XLA Modules:
  0.0 1221.6 jit_solution(15383758015206890385)
XLA Ops:
  11.6 28.7 %all-gather.6.cloned.1.call-done = bf16[512,1024]{1,0:T(8,128)(2,1)} async-done(((bf16[128,1024]{1,0:T(8,128)(2,1)}), bf16[512,1024]{1,0:T(8,128)(2,1)}) %all-gather.6.cloned.1.call-update) | async-done | bytes 1048592 | tf_op jit(solution)/shard_map/all_gather | solution.py:157
  40.3 5.1 multiply_convert_fusion.2
  45.4 23.9 %all-gather.8.cloned.1.call-done = bf16[512,1024]{1,0:T(8,128)(2,1)} async-done(((bf16[128,1024]{1,0:T(8,128)(2,1)}), bf16[512,1024]{1,0:T(8,128)(2,1)}) %all-gather.8.cloned.1.call-update) | async-done | bytes 1048592 | tf_op jit(solution)/shard_map/all_gather | solution.py:158
  69.3 4.1 convolution_convert_fusion.10
  74.3 17.5 %all_gather.29 = bf16[512,3,256]{0,2,1:T(8,128)(2,1)S(1)} all-gather(bf16[128,3,256]{0,2,1:T(8,128)(2,1)S(1)} %copy.27), channel_id=1, replica_groups=mesh['fsdp'=4,'ctx'=4,'tp'=2] {'fsdp'}, dimensions={0}, use_global_device_ids=true | all-gather | bytes 983040 | tf_op jit(solution)/shard_map/all_gather | solution.py:159
  91.8 21.4 %all-reduce.20.cloned.1.call-done = bf16[1024,512]{1,0:T(8,128)(2,1)} async-done(((bf16[1024,512]{1,0:T(8,128)(2,1)}), bf16[1024,512]{1,0:T(8,128)(2,1)}) %all-reduce.20.cloned.1.call-update) | async-done | bytes 1048592 | tf_op jit(solution)/shard_map/psum | solution.py:51
  119.6 14.3 %all_gather.31 = bf16[512,256]{1,0:T(8,128)(2,1)S(1)} all-gather(bf16[128,256]{1,0:T(8,128)(2,1)S(1)} %copy-done.69), channel_id=1, replica_groups=mesh['fsdp'=4,'ctx'=4,'tp'=2] {'fsdp'}, dimensions={0}, use_global_device_ids=true | all-gather | bytes 327680 | tf_op jit(solution)/shard_map/all_gather | solution.py:160
  134.0 19.6 %all-gather.10.cloned.1.call-done = bf16[1,4096,512]{1,2,0:T(8,128)(2,1)} async-done(((bf16[1,1024,512]{1,2,0:T(8,128)(2,1)}), bf16[1,4096,512]{1,2,0:T(8,128)(2,1)}) %all-gather.10.cloned.1.call-update) | async-done | bytes 4194320 | tf_op jit(solution)/shard_map/all_gather | solution.py:190
  153.5 4.1 fusion.240
  157.6 23.1 %select_reduce_fusion = (f32[4,1024]{1,0:T(4,128)S(1)}, f32[4,1024,4096]{2,1,0:T(8,128)}) fusion(pred[4096]{0:T(1024)(128)(4,1)S(1)} %iota_compare_fusion, bf16[4096,4,64]{0,2,1:T(8,128)(2,1)S(1)} %bitcast.233, f32[1024,4,32]{0,2,1:T(8,128)S(1)} %get-tuple-element.156, f32[1024,4,32]{0,2,1:T(8,128)S(1)} %get-tuple-element.155), kind=kOutput, calls=%fused_computation.6 | convolution fusion | flops 2181820416 | bytes 70275072 | tf_op jit(solution)/shard_map/while/body/eval_jaxpr/fhe,lhe->hfl/dot_general | solution.py:97
  180.8 21.4 %fusion = f32[4,1024]{1,0:T(4,128)S(1)} fusion(f32[4,1024,4096]{2,1,0:T(8,128)} %get-tuple-element.214, f32[4,1024]{1,0:T(4,128)S(1)} %get-tuple-element.213, pred[4096]{0:T(1024)(128)(4,1)S(1)} %iota_compare_fusion), kind=kLoop, calls=%fused_computation.5 | loop fusion | flops 50327552 | bytes 67145728 | tf_op jit(solution)/shard_map/while/body/eval_jaxpr/reduce_sum | solution.py:108
  202.2 24.0 %fusion.33 = bf16[4,64,1024]{2,1,0:T(8,128)(2,1)S(1)} fusion(bf16[4096,4,64]{0,2,1:T(8,128)(2,1)S(1)} %bitcast.241, f32[4,1024,4096]{2,1,0:T(8,128)} %get-tuple-element.214, f32[4,1024]{1,0:T(4,128)S(1)} %fusion, f32[4,1024]{1,0:T(4,128)S(1)} %get-tuple-element.213, pred[4096]{0:T(1024)(128)(4,1)S(1)} %iota_compare_fusion), kind=kOutput, calls=%fused_computation.222 | convolution fusion | flops 2214854656 | bytes 69767168 | tf_op jit(solution)/shard_map/while/body/eval_jaxpr/hfl,lhe->fhe/dot_general | solution.py:110
  227.8 16.0 %all_gather.32 = bf16[512,2,256]{2,0,1:T(8,128)(2,1)S(1)} all-gather(bf16[128,2,256]{2,0,1:T(8,128)(2,1)S(1)} %copy.28), channel_id=1, replica_groups=mesh['fsdp'=4,'ctx'=4,'tp'=2] {'fsdp'}, dimensions={0}, use_global_device_ids=true | all-gather | bytes 655360 | tf_op jit(solution)/shard_map/all_gather | solution.py:161
  245.1 22.8 %all-reduce.22.cloned.1.call-done = bf16[1024,512]{1,0:T(8,128)(2,1)} async-done(((bf16[1024,512]{1,0:T(8,128)(2,1)}), bf16[1024,512]{1,0:T(8,128)(2,1)}) %all-reduce.22.cloned.1.call-update) | async-done | bytes 1048592 | tf_op jit(solution)/shard_map/psum | solution.py:51
  276.0 15.4 %all_gather.33 = bf16[512,256]{1,0:T(8,128)(2,1)} all-gather(bf16[128,256]{1,0:T(8,128)(2,1)S(1)} %copy-done.70), channel_id=1, replica_groups=mesh['fsdp'=4,'ctx'=4,'tp'=2] {'fsdp'}, dimensions={0}, use_global_device_ids=true | all-gather | bytes 327680 | tf_op jit(solution)/shard_map/all_gather | solution.py:162
  292.3 9.3 fusion.64
  301.6 32.1 %all-reduce.8 = (f32[256]{0:T(256)S(1)}, f32[]{:T(128)}, f32[256]{0:T(256)S(1)}) all-reduce(f32[256]{0:T(256)} %get-tuple-element.109, f32[]{:T(128)} %fusion.202, f32[256]{0:T(256)} %get-tuple-element.108), channel_id=1, replica_groups=mesh['fsdp'=4,'ctx'=4,'tp'=2] {'fsdp','ctx'}, use_global_device_ids=true, to_apply=%region_11.12 | all-reduce | flops 513 | bytes 4104 | tf_op jit(solution)/shard_map/psum | solution.py:211
  334.9 2.8 convolution_convert_fusion.8
  339.3 35.0 %all-reduce.24.cloned.1.call-done = bf16[1024,512]{1,0:T(8,128)(2,1)} async-done(((bf16[1024,512]{1,0:T(8,128)(2,1)}), bf16[1024,512]{1,0:T(8,128)(2,1)}) %all-reduce.24.cloned.1.call-update) | async-done | bytes 1048592 | tf_op jit(solution)/shard_map/psum | solution.py:51
  377.6 26.3 %all-gather.12.cloned.1.call-done = bf16[512,1024]{1,0:T(8,128)(2,1)} async-done(((bf16[128,1024]{1,0:T(8,128)(2,1)}), bf16[512,1024]{1,0:T(8,128)(2,1)}) %all-gather.12.cloned.1.call-update) | async-done | bytes 1048592 | tf_op jit(solution)/shard_map/all_gather | solution.py:163
  403.9 6.1 multiply_convert_fusion.1
  410.0 22.9 %all-gather.14.cloned.1.call-done = bf16[512,1024]{1,0:T(8,128)(2,1)} async-done(((bf16[128,1024]{1,0:T(8,128)(2,1)}), bf16[512,1024]{1,0:T(8,128)(2,1)}) %all-gather.14.cloned.1.call-update) | async-done | bytes 1048592 | tf_op jit(solution)/shard_map/all_gather | solution.py:164
  432.9 4.1 convolution_convert_fusion.7
  437.0 39.6 %all-reduce.26.cloned.1.call-done = bf16[1024,512]{1,0:T(8,128)(2,1)} async-done(((bf16[1024,512]{1,0:T(8,128)(2,1)}), bf16[1024,512]{1,0:T(8,128)(2,1)}) %all-reduce.26.cloned.1.call-update) | async-done | bytes 1048592 | tf_op jit(solution)/shard_map/psum | solution.py:51
  485.5 2.5 fusion.11
  492.0 40.0 %all-reduce.28.cloned.1.call-done = bf16[1024,512]{1,0:T(8,128)(2,1)} async-done(((bf16[1024,512]{1,0:T(8,128)(2,1)}), bf16[1024,512]{1,0:T(8,128)(2,1)}) %all-reduce.28.cloned.1.call-update) | async-done | bytes 1048592 | tf_op jit(solution)/shard_map/psum | solution.py:51
  532.0 2.6 fusion.26
  542.2 33.7 %all-reduce.7 = (f32[256]{0:T(256)}, f32[256]{0:T(256)}) all-reduce(f32[256]{0:T(256)} %get-tuple-element.217, f32[256]{0:T(256)} %reduce_sum.647), channel_id=1, replica_groups=mesh['fsdp'=4,'ctx'=4,'tp'=2] {'fsdp','ctx'}, use_global_device_ids=true, to_apply=%region_30.31 | all-reduce | flops 512 | bytes 4096 | tf_op jit(solution)/shard_map/psum | solution.py:241
  577.5 5.4 fusion.115
  584.2 3.0 collective-permute-start.3
  588.1 9.3 fusion.67
  600.7 38.1 %all-reduce.30.cloned.1.call-done = bf16[1024,512]{1,0:T(8,128)(2,1)} async-done(((bf16[1024,512]{1,0:T(8,128)(2,1)}), bf16[1024,512]{1,0:T(8,128)(2,1)}) %all-reduce.30.cloned.1.call-update) | async-done | bytes 1048592 | tf_op jit(solution)/shard_map/psum | solution.py:51
  640.7 2.3 fusion.28
  645.5 23.9 %fusion.6 = bf16[4,64,4096]{2,1,0:T(8,128)(2,1)S(1)} fusion(bf16[1024,4,64]{0,2,1:T(8,128)(2,1)S(1)} %bitcast.237, f32[4,1024,4096]{2,1,0:T(8,128)} %get-tuple-element.214, f32[4,1024]{1,0:T(4,128)S(1)} %log_add_fusion, pred[4096]{0:T(1024)(128)(4,1)S(1)} %iota_compare_fusion), kind=kOutput, calls=%fused_computation.45 | convolution fusion | flops 2198863872 | bytes 69750784 | tf_op jit(solution)/shard_map/while/body/eval_jaxpr/hfl,fhe->lhe/dot_general | solution.py:124
  669.4 45.1 %multiply_reduce_fusion = (f32[4,1024]{1,0:T(4,128)S(1)}, f32[4,1024,4096]{2,1,0:T(8,128)}) fusion(f32[4,1024,4096]{2,1,0:T(8,128)} %get-tuple-element.214, f32[4,1024]{1,0:T(4,128)S(1)} %log_add_fusion, pred[4096]{0:T(1024)(128)(4,1)S(1)} %iota_compare_fusion, bf16[1024,4,64]{0,2,1:T(8,128)(2,1)S(1)} %bitcast.238, bf16[4096,4,64]{0,2,1:T(8,128)(2,1)S(1)} %bitcast.242), kind=kOutput, calls=%fused_computation.1 | convolution fusion | flops 2214588416 | bytes 136876032 | tf_op jit(solution)/shard_map/while/body/eval_jaxpr/fhe,lhe->hfl/dot_general | solution.py:119
  714.5 2.5 copy.30
  717.0 52.7 %multiply_convert_fusion = bf16[4,1024,4096]{2,1,0:T(8,128)(2,1)} fusion(f32[4,1024,4096]{2,1,0:T(8,128)} %get-tuple-element.220, f32[4,1024,4096]{2,1,0:T(8,128)} %get-tuple-element.214, f32[4,1024]{1,0:T(4,128)S(1)} %get-tuple-element.219, f32[4,1024]{1,0:T(4,128)S(1)} %log_add_fusion, pred[4096]{0:T(1024)(128)(4,1)S(1)} %iota_compare_fusion), kind=kLoop, calls=%fused_computation | loop fusion | flops 83886080 | bytes 167809024 | tf_op jit(solution)/shard_map/while/body/eval_jaxpr/convert_element_type | solution.py:121
  769.7 13.8 %convolution_convert_fusion = bf16[4,64,4096]{2,1,0:T(8,128)(2,1)S(1)} fusion(bf16[4,1024,4096]{2,1,0:T(8,128)(2,1)} %multiply_convert_fusion, f32[1024,4,32]{0,2,1:T(8,128)S(1)} %copy-done.36, f32[1024,4,32]{0,2,1:T(8,128)S(1)} %copy-done.34), kind=kOutput, calls=%fused_computation.46 | convolution fusion | flops 2149318656 | bytes 36700160 | tf_op jit(solution)/shard_map/while/body/eval_jaxpr/hfl,fhe->lhe/dot_general | solution.py:123
  783.5 2.5 copy.29
  786.0 4.5 pad_maximum_fusion
  792.1 17.0 %fusion.32 = f32[1,1024,4,64]{1,3,2,0:T(8,128)S(1)} fusion(bf16[4096,4,64]{0,2,1:T(8,128)(2,1)S(1)} %bitcast.234, bf16[4,1024,4096]{2,1,0:T(8,128)(2,1)} %multiply_convert_fusion), kind=kOutput, calls=%fused_computation.188 | convolution fusion | flops 2147745792 | bytes 36700160 | tf_op jit(solution)/shard_map/while/body/eval_jaxpr/hfl,lhe->fhe/dot_general | solution.py:122
  809.1 26.2 %reduce-scatter.10.cloned.1.call-done = bf16[1,1024,512]{2,1,0:T(8,128)(2,1)} async-done(((bf16[1,4096,512]{2,1,0:T(8,128)(2,1)}), bf16[1,1024,512]{2,1,0:T(8,128)(2,1)}) %reduce-scatter.10.cloned.1.call-update) | async-done | bytes 1048592 | tf_op jit(solution)/shard_map/reduce_scatter | solution.py:283
  840.2 3.4 bitcast_convert_fusion
  843.6 40.2 %all-reduce.32.cloned.1.call-done = bf16[1024,512]{1,0:T(8,128)(2,1)} async-done(((bf16[1024,512]{1,0:T(8,128)(2,1)}), bf16[1024,512]{1,0:T(8,128)(2,1)}) %all-reduce.32.cloned.1.call-update) | async-done | bytes 1048592 | tf_op jit(solution)/shard_map/psum | solution.py:51
  894.3 2.3 convolution_convert_fusion.5
  896.7 3.1 convolution_convert_fusion.14
  900.0 4.0 convolution_convert_fusion.2
  904.1 4.7 convolution_convert_fusion.1
  909.1 3.4 convolution_convert_fusion.13
  912.6 2.9 convolution_convert_fusion.15
  915.7 3.3 convolution_convert_fusion.11
  919.2 4.7 convolution_convert_fusion.4
  924.0 4.0 convolution_convert_fusion.3
  933.3 3.6 all-reduce.34.cloned.1.call-done
  938.8 20.8 %reduce-scatter.22.cloned.1.call-done = bf16[128,256]{1,0:T(8,128)(2,1)} async-done(((bf16[512,256]{1,0:T(8,128)(2,1)}), bf16[128,256]{1,0:T(8,128)(2,1)}) %reduce-scatter.22.cloned.1.call-update) | async-done | bytes 65552 | tf_op jit(solution)/shard_map/reduce_scatter | solution.py:334
  959.5 27.7 %reduce-scatter.24.cloned.1.call-done = bf16[128,1024]{1,0:T(8,128)(2,1)} async-done(((bf16[512,1024]{1,0:T(8,128)(2,1)}), bf16[128,1024]{1,0:T(8,128)(2,1)}) %reduce-scatter.24.cloned.1.call-update) | async-done | bytes 262160 | tf_op jit(solution)/shard_map/reduce_scatter | solution.py:337
  987.2 27.9 %reduce-scatter.26.cloned.1.call-done = bf16[128,1024]{1,0:T(8,128)(2,1)} async-done(((bf16[512,1024]{1,0:T(8,128)(2,1)}), bf16[128,1024]{1,0:T(8,128)(2,1)}) %reduce-scatter.26.cloned.1.call-update) | async-done | bytes 262160 | tf_op jit(solution)/shard_map/reduce_scatter | solution.py:340
  1015.2 22.5 %reduce-scatter.20.cloned.1.call-done = bf16[128,2,256]{2,0,1:T(8,128)(2,1)} async-done(((bf16[512,2,256]{2,0,1:T(8,128)(2,1)}), bf16[128,2,256]{2,0,1:T(8,128)(2,1)}) %reduce-scatter.20.cloned.1.call-update) | async-done | bytes 131088 | tf_op jit(solution)/shard_map/reduce_scatter | solution.py:331
  1037.7 21.1 %reduce-scatter.18.cloned.1.call-done = bf16[128,256]{1,0:T(8,128)(2,1)} async-done(((bf16[512,256]{1,0:T(8,128)(2,1)}), bf16[128,256]{1,0:T(8,128)(2,1)}) %reduce-scatter.18.cloned.1.call-update) | async-done | bytes 65552 | tf_op jit(solution)/shard_map/reduce_scatter | solution.py:328
  1058.8 23.5 %reduce-scatter.16.cloned.1.call-done = bf16[128,3,256]{2,0,1:T(8,128)(2,1)} async-done(((bf16[512,3,256]{2,0,1:T(8,128)(2,1)}), bf16[128,3,256]{2,0,1:T(8,128)(2,1)}) %reduce-scatter.16.cloned.1.call-update) | async-done | bytes 196624 | tf_op jit(solution)/shard_map/reduce_scatter | solution.py:325
  1082.3 29.1 %reduce-scatter.12.cloned.1.call-done = bf16[128,1024]{1,0:T(8,128)(2,1)} async-done(((bf16[512,1024]{1,0:T(8,128)(2,1)}), bf16[128,1024]{1,0:T(8,128)(2,1)}) %reduce-scatter.12.cloned.1.call-update) | async-done | bytes 262160 | tf_op jit(solution)/shard_map/reduce_scatter | solution.py:319
  1111.5 28.1 %reduce-scatter.14.cloned.1.call-done = bf16[128,1024]{1,0:T(8,128)(2,1)} async-done(((bf16[512,1024]{1,0:T(8,128)(2,1)}), bf16[128,1024]{1,0:T(8,128)(2,1)}) %reduce-scatter.14.cloned.1.call-update) | async-done | bytes 262160 | tf_op jit(solution)/shard_map/reduce_scatter | solution.py:322
  1141.0 59.7 %all-reduce.6 = (f32[5,512]{1,0:T(8,128)}, f32[31,256]{1,0:T(8,128)}) all-reduce(f32[5,512]{1,0:T(8,128)S(1)} %stack.128, f32[31,256]{1,0:T(8,128)S(1)} %stack.160), channel_id=1, replica_groups=mesh['fsdp'=4,'ctx'=4,'tp'=2] {'fsdp','ctx'}, use_global_device_ids=true, to_apply=%region_47.48 | all-reduce | flops 10496 | bytes 83968 | tf_op jit(solution)/shard_map/psum | solution.py:307
  1200.7 3.3 add_bitcast_fusion
  (449 shorter events, 96.4 us)
Async XLA Ops:
  7.2 33.1 %all-gather.6.cloned.1.call-start = ((), (), s32[]{:S(2)}) async-start(), calls=%async_computation.9 | async-start | bytes 1310720 | tf_op jit(solution)/shard_map/all_gather | solution.py:157
  7.9 61.3 %all-gather.8.cloned.1.call-start = ((), (), s32[]{:S(2)}) async-start(), calls=%async_computation.10 | async-start | bytes 1310720 | tf_op jit(solution)/shard_map/all_gather | solution.py:158
  8.7 104.4 %all-reduce.20.cloned.1.call-start = ((), (), s32[]{:S(2)}) async-start(), calls=%async_computation.11 | async-start | bytes 2097152 | tf_op jit(solution)/shard_map/psum | solution.py:51
  10.6 34.8 %copy-start.65 = (f32[1024]{0:T(1024)}, f32[1024]{0:T(1024)S(1)}, u32[]{:S(2)}) copy-start(f32[1024]{0:T(1024)S(1)} %broadcast_multiply_fusion.4) | copy-start | bytes 12292
  11.0 34.4 %copy-start.83 = (f32[1024]{0:T(1024)}, f32[1024]{0:T(1024)S(1)}, u32[]{:S(2)}) copy-start(f32[1024]{0:T(1024)S(1)} %multiply_reduce_fusion.6) | copy-start | bytes 12292
  11.6 104.2 %copy-start.75 = (f32[1,512]{1,0:T(1,128)}, f32[1,512]{1,0:T(1,128)S(1)}, u32[]{:S(2)}) copy-start(f32[1,512]{1,0:T(1,128)S(1)} %get-tuple-element.202) | copy-start | bytes 6148
  11.6 631.4 %copy-start.77 = (f32[1,512]{1,0:T(1,128)}, f32[1,512]{1,0:T(1,128)S(1)}, u32[]{:S(2)}) copy-start(f32[1,512]{1,0:T(1,128)S(1)} %get-tuple-element.201) | copy-start | bytes 6148
  73.4 80.1 %all-gather.10.cloned.1.call-start = ((), (), s32[]{:S(2)}) async-start(), calls=%async_computation.12 | async-start | bytes 5242880 | tf_op jit(solution)/shard_map/all_gather | solution.py:190
  74.2 43.1 %copy-start.43 = (f32[1024,32]{0,1:T(8,128)}, f32[1024,32]{0,1:T(8,128)S(1)}, u32[]{:S(2)}) copy-start(f32[1024,32]{0,1:T(8,128)S(1)} %get-tuple-element.205) | copy-start | bytes 393220
  74.2 43.1 %copy-start.45 = (f32[1024,32]{0,1:T(8,128)}, f32[1024,32]{0,1:T(8,128)S(1)}, u32[]{:S(2)}) copy-start(f32[1024,32]{0,1:T(8,128)S(1)} %get-tuple-element.206) | copy-start | bytes 393220
  117.6 40.0 %copy-start.33 = (f32[1024,4,32]{0,2,1:T(8,128)}, f32[1024,4,32]{0,2,1:T(8,128)S(1)}, u32[]{:S(2)}) copy-start(f32[1024,4,32]{0,2,1:T(8,128)S(1)} %get-tuple-element.155) | copy-start | bytes 1572868
  117.6 40.0 %copy-start.35 = (f32[1024,4,32]{0,2,1:T(8,128)}, f32[1024,4,32]{0,2,1:T(8,128)S(1)}, u32[]{:S(2)}) copy-start(f32[1024,4,32]{0,2,1:T(8,128)S(1)} %get-tuple-element.156) | copy-start | bytes 1572868
  118.9 149.0 %all-reduce.22.cloned.1.call-start = ((), (), s32[]{:S(2)}) async-start(), calls=%async_computation.13 | async-start | bytes 2097152 | tf_op jit(solution)/shard_map/psum | solution.py:51
  226.2 43.9 %copy-start.41 = (bf16[4,64,1024]{2,1,0:T(8,128)(2,1)}, bf16[4,64,1024]{2,1,0:T(8,128)(2,1)S(1)}, u32[]{:S(2)}) copy-start(bf16[4,64,1024]{2,1,0:T(8,128)(2,1)S(1)} %fusion.33) | copy-start | bytes 1572868
  227.7 146.6 %all-reduce.24.cloned.1.call-start = ((), (), s32[]{:S(2)}) async-start(), calls=%async_computation.14 | async-start | bytes 2097152 | tf_op jit(solution)/shard_map/psum | solution.py:51
  244.4 331.5 %copy-start.95 = (f32[1,256]{1,0:T(1,128)}, f32[1,256]{1,0:T(1,128)S(1)}, u32[]{:S(2)}) copy-start(f32[1,256]{1,0:T(1,128)S(1)} %get-tuple-element.209) | copy-start | bytes 3076
  245.1 47.0 %copy-start.97 = (f32[1,256]{1,0:T(1,128)}, f32[1,256]{1,0:T(1,128)S(1)}, u32[]{:S(2)}) copy-start(f32[1,256]{1,0:T(1,128)S(1)} %get-tuple-element.170) | copy-start | bytes 3076
  245.1 47.0 %copy-start.99 = (f32[1,256]{1,0:T(1,128)}, f32[1,256]{1,0:T(1,128)S(1)}, u32[]{:S(2)}) copy-start(f32[1,256]{1,0:T(1,128)S(1)} %get-tuple-element.171) | copy-start | bytes 3076
  245.1 47.0 %copy-start.101 = (f32[1,256]{1,0:T(1,128)}, f32[1,256]{1,0:T(1,128)S(1)}, u32[]{:S(2)}) copy-start(f32[1,256]{1,0:T(1,128)S(1)} %get-tuple-element.172) | copy-start | bytes 3076
  245.1 47.0 %copy-start.103 = (f32[1,256]{1,0:T(1,128)}, f32[1,256]{1,0:T(1,128)S(1)}, u32[]{:S(2)}) copy-start(f32[1,256]{1,0:T(1,128)S(1)} %get-tuple-element.173) | copy-start | bytes 3076
  270.1 372.9 %copy-start = (f32[1024,512]{1,0:T(8,128)}, f32[1024,512]{1,0:T(8,128)S(1)}, u32[]{:S(2)}) copy-start(f32[1024,512]{1,0:T(8,128)S(1)} %get-tuple-element.143) | copy-start | bytes 6291460
  270.1 372.9 %copy-start.58 = (f32[1024]{0:T(1024)}, f32[1024]{0:T(1024)S(1)}, u32[]{:S(2)}) copy-start(f32[1024]{0:T(1024)S(1)} %broadcast_multiply_fusion.2) | copy-start | bytes 12292
  270.6 372.4 %copy-start.73 = (f32[1024]{0:T(1024)}, f32[1024]{0:T(1024)S(1)}, u32[]{:S(2)}) copy-start(f32[1024]{0:T(1024)S(1)} %fusion.199) | copy-start | bytes 12292
  273.1 304.3 %copy-start.14 = (bf16[1,1024,256]{2,1,0:T(8,128)(2,1)}, bf16[1,1024,256]{2,1,0:T(8,128)(2,1)S(1)}, u32[]{:S(2)}) copy-start(bf16[1,1024,256]{2,1,0:T(8,128)(2,1)S(1)} %fusion.127) | copy-start | bytes 1572868
  273.2 18.9 %collective-permute-start = (bf16[1,15,256]{2,1,0:T(8,128)(2,1)S(1)}, bf16[1,15,256]{2,1,0:T(8,128)(2,1)S(1)}, u32[]{:S(2)}, u32[]{:S(2)}) collective-permute-start(bf16[1,15,256]{2,1,0:T(8,128)(2,1)S(1)} %get-tuple-element.163), channel_id=1, source_target_pairs={{0,2},{2,4},{4,6},{1,3},{3,5},{5,7},{8,10},{10,12},{12,14},{9,11},... | collective-permute-start | bytes 23048 | tf_op jit(solution)/shard_map/ppermute | solution.py:20
  274.7 17.4 %collective-permute-start.1 = (bf16[1,15,256]{2,1,0:T(8,128)(2,1)S(1)}, bf16[1,15,256]{2,1,0:T(8,128)(2,1)S(1)}, u32[]{:S(2)}, u32[]{:S(2)}) collective-permute-start(bf16[1,15,256]{2,1,0:T(8,128)(2,1)S(1)} %get-tuple-element.164), channel_id=1, source_target_pairs={{2,0},{4,2},{6,4},{3,1},{5,3},{7,5},{10,8},{12,10},{14,12},{11,9},... | collective-permute-start | bytes 23048 | tf_op jit(solution)/shard_map/ppermute | solution.py:22
  292.1 45.6 %copy-start.62 = (bf16[1,15,256]{2,1,0:T(8,128)(2,1)}, bf16[1,15,256]{2,1,0:T(8,128)(2,1)S(1)}, u32[]{:S(2)}) copy-start(bf16[1,15,256]{2,1,0:T(8,128)(2,1)S(1)} %collective-permute-done) | copy-start | bytes 23044
  292.1 285.4 %copy-start.60 = (bf16[1,15,256]{2,1,0:T(8,128)(2,1)}, bf16[1,15,256]{2,1,0:T(8,128)(2,1)S(1)}, u32[]{:S(2)}) copy-start(bf16[1,15,256]{2,1,0:T(8,128)(2,1)S(1)} %collective-permute-done.1) | copy-start | bytes 23044
  337.7 66.2 %all-gather.12.cloned.1.call-start = ((), (), s32[]{:S(2)}) async-start(), calls=%async_computation.15 | async-start | bytes 1310720 | tf_op jit(solution)/shard_map/all_gather | solution.py:163
  338.5 94.4 %all-gather.14.cloned.1.call-start = ((), (), s32[]{:S(2)}) async-start(), calls=%async_computation.16 | async-start | bytes 1310720 | tf_op jit(solution)/shard_map/all_gather | solution.py:164
  339.2 137.4 %all-reduce.26.cloned.1.call-start = ((), (), s32[]{:S(2)}) async-start(), calls=%async_computation.17 | async-start | bytes 2097152 | tf_op jit(solution)/shard_map/psum | solution.py:51
  375.8 160.8 %copy-start.67 = (f32[1024]{0:T(1024)}, f32[1024]{0:T(1024)S(1)}, u32[]{:S(2)}) copy-start(f32[1024]{0:T(1024)S(1)} %broadcast_multiply_fusion.1) | copy-start | bytes 12292
  377.6 159.1 %copy-start.81 = (f32[1024]{0:T(1024)}, f32[1024]{0:T(1024)S(1)}, u32[]{:S(2)}) copy-start(f32[1024]{0:T(1024)S(1)} %fusion.200) | copy-start | bytes 12292
  437.0 95.0 %all-reduce.28.cloned.1.call-start = ((), (), s32[]{:S(2)}) async-start(), calls=%async_computation.18 | async-start | bytes 2097152 | tf_op jit(solution)/shard_map/psum | solution.py:51
  483.8 52.9 %copy-start.93 = (f32[1024]{0:T(1024)}, f32[1024]{0:T(1024)S(1)}, u32[]{:S(2)}) copy-start(f32[1024]{0:T(1024)S(1)} %negate_multiply_fusion.4) | copy-start | bytes 12292
  491.7 147.0 %all-reduce.30.cloned.1.call-start = ((), (), s32[]{:S(2)}) async-start(), calls=%async_computation.19 | async-start | bytes 2097152 | tf_op jit(solution)/shard_map/psum | solution.py:51
  540.2 47.8 %copy-start.98 = (f32[1,256]{1,0:T(1,128)S(1)}, f32[1,256]{1,0:T(1,128)}, u32[]{:S(2)}) copy-start(f32[1,256]{1,0:T(1,128)} %copy-done.97) | copy-start | bytes 3076
  540.2 47.8 %copy-start.100 = (f32[1,256]{1,0:T(1,128)S(1)}, f32[1,256]{1,0:T(1,128)}, u32[]{:S(2)}) copy-start(f32[1,256]{1,0:T(1,128)} %copy-done.99) | copy-start | bytes 3076
  540.2 47.8 %copy-start.102 = (f32[1,256]{1,0:T(1,128)S(1)}, f32[1,256]{1,0:T(1,128)}, u32[]{:S(2)}) copy-start(f32[1,256]{1,0:T(1,128)} %copy-done.101) | copy-start | bytes 3076
  540.2 47.8 %copy-start.104 = (f32[1,256]{1,0:T(1,128)S(1)}, f32[1,256]{1,0:T(1,128)}, u32[]{:S(2)}) copy-start(f32[1,256]{1,0:T(1,128)} %copy-done.103) | copy-start | bytes 3076
  540.2 47.8 %copy-start.106 = (f32[1,256]{1,0:T(1,128)S(1)}, f32[1,256]{1,0:T(1,128)}, u32[]{:S(2)}) copy-start(f32[1,256]{1,0:T(1,128)} %get-tuple-element.174) | copy-start | bytes 3076
  540.3 47.8 %copy-start.108 = (f32[1,256]{1,0:T(1,128)S(1)}, f32[1,256]{1,0:T(1,128)}, u32[]{:S(2)}) copy-start(f32[1,256]{1,0:T(1,128)} %get-tuple-element.175) | copy-start | bytes 3076
  582.9 4.3 collective-permute-start.2
  584.2 3.8 collective-permute-start.3
  600.6 234.7 %reduce-scatter.10.cloned.1.call-start = ((), (), s32[]{:S(2)}) async-start(), calls=%async_computation.20 | async-start | bytes 5242880 | tf_op jit(solution)/shard_map/reduce_scatter | solution.py:283
  717.0 52.7 %copy-start.34 = (f32[1024,4,32]{0,2,1:T(8,128)S(1)}, f32[1024,4,32]{0,2,1:T(8,128)}, u32[]{:S(2)}) copy-start(f32[1024,4,32]{0,2,1:T(8,128)} %copy-done.33) | copy-start | bytes 1572868
  717.0 52.7 %copy-start.36 = (f32[1024,4,32]{0,2,1:T(8,128)S(1)}, f32[1024,4,32]{0,2,1:T(8,128)}, u32[]{:S(2)}) copy-start(f32[1024,4,32]{0,2,1:T(8,128)} %copy-done.35) | copy-start | bytes 1572868
  790.5 93.3 %all-reduce.32.cloned.1.call-start = ((), (), s32[]{:S(2)}) async-start(), calls=%async_computation.21 | async-start | bytes 2097152 | tf_op jit(solution)/shard_map/psum | solution.py:51
  840.2 43.7 %copy-start.3 = (f32[1024,512]{1,0:T(8,128)S(1)}, f32[1024,512]{1,0:T(8,128)}, u32[]{:S(2)}) copy-start(f32[1024,512]{1,0:T(8,128)} %copy-done.2) | copy-start | bytes 6291460
  840.2 43.7 %copy-start.57 = (f32[1024]{0:T(1024)S(1)}, f32[1024]{0:T(1024)}, u32[]{:S(2)}) copy-start(f32[1024]{0:T(1024)} %copy-done.56) | copy-start | bytes 12292
  840.2 43.7 %copy-start.76 = (f32[1,512]{1,0:T(1,128)S(1)}, f32[1,512]{1,0:T(1,128)}, u32[]{:S(2)}) copy-start(f32[1,512]{1,0:T(1,128)} %copy-done.75) | copy-start | bytes 6148
  843.6 42.2 %copy-start.86 = (f32[1024]{0:T(1024)S(1)}, f32[1024]{0:T(1024)}, u32[]{:S(2)}) copy-start(f32[1024]{0:T(1024)} %copy-done.85) | copy-start | bytes 12292
  843.6 42.3 %copy-start.72 = (f32[1024]{0:T(1024)S(1)}, f32[1024]{0:T(1024)}, u32[]{:S(2)}) copy-start(f32[1024]{0:T(1024)} %copy-done.71) | copy-start | bytes 12292
  843.6 93.3 %all-reduce.34.cloned.1.call-start = ((), (), s32[]{:S(2)}) async-start(), calls=%async_computation.22 | async-start | bytes 2097152 | tf_op jit(solution)/shard_map/psum | solution.py:51
  896.6 62.9 %reduce-scatter.22.cloned.1.call-start = ((), (), s32[]{:S(2)}) async-start(), calls=%async_computation.28 | async-start | bytes 327680 | tf_op jit(solution)/shard_map/reduce_scatter | solution.py:334
  899.9 87.4 %reduce-scatter.24.cloned.1.call-start = ((), (), s32[]{:S(2)}) async-start(), calls=%async_computation.29 | async-start | bytes 1310720 | tf_op jit(solution)/shard_map/reduce_scatter | solution.py:337
  904.0 111.2 %reduce-scatter.26.cloned.1.call-start = ((), (), s32[]{:S(2)}) async-start(), calls=%async_computation.30 | async-start | bytes 1310720 | tf_op jit(solution)/shard_map/reduce_scatter | solution.py:340
  908.8 128.9 %reduce-scatter.20.cloned.1.call-start = ((), (), s32[]{:S(2)}) async-start(), calls=%async_computation.27 | async-start | bytes 655360 | tf_op jit(solution)/shard_map/reduce_scatter | solution.py:331
  912.6 146.2 %reduce-scatter.18.cloned.1.call-start = ((), (), s32[]{:S(2)}) async-start(), calls=%async_computation.26 | async-start | bytes 327680 | tf_op jit(solution)/shard_map/reduce_scatter | solution.py:328
  915.6 166.7 %reduce-scatter.16.cloned.1.call-start = ((), (), s32[]{:S(2)}) async-start(), calls=%async_computation.25 | async-start | bytes 983040 | tf_op jit(solution)/shard_map/reduce_scatter | solution.py:325
  919.1 192.4 %reduce-scatter.12.cloned.1.call-start = ((), (), s32[]{:S(2)}) async-start(), calls=%async_computation.23 | async-start | bytes 1310720 | tf_op jit(solution)/shard_map/reduce_scatter | solution.py:319
  924.0 215.6 %reduce-scatter.14.cloned.1.call-start = ((), (), s32[]{:S(2)}) async-start(), calls=%async_computation.24 | async-start | bytes 1310720 | tf_op jit(solution)/shard_map/reduce_scatter | solution.py:322
  928.1 275.8 %all-reduce.36.cloned.1.call-start = ((), (), s32[]{:S(2)}) async-start(), calls=%async_computation.31 | async-start | bytes 3014656 | tf_op jit(solution)/shard_map/psum | solution.py:349
  936.8 202.8 %copy-start.20 = (bf16[1024,512]{1,0:T(8,128)(2,1)S(1)}, bf16[1024,512]{1,0:T(8,128)(2,1)}, u32[]{:S(2)}) copy-start(bf16[1024,512]{1,0:T(8,128)(2,1)} %all-reduce.34.cloned.1.call-done) | copy-start | bytes 3145732
  (113 other events, 850.9 us)
Sparse Core Ops, SparseCore 0:
  9.6 30.6 all-gather.5
  41.9 27.3 all-gather.7
  73.6 39.5 all-reduce.19
  119.1 34.4 all-gather.9
  227.8 40.0 all-reduce.21
  337.8 36.4 all-reduce.23
  375.9 27.9 all-gather.11
  405.5 27.3 all-gather.13
  437.1 39.4 all-reduce.25
  491.8 40.0 all-reduce.27
  600.7 38.0 all-reduce.29
  790.6 44.5 reduce-scatter.9
  843.7 40.1 all-reduce.31
  896.7 40.0 all-reduce.33
  939.5 19.9 reduce-scatter.21
  961.7 25.5 reduce-scatter.23
  989.4 25.7 reduce-scatter.25
  1017.3 20.3 reduce-scatter.19
  1040.5 18.2 reduce-scatter.17
  1060.9 21.3 reduce-scatter.15
  1084.6 26.7 reduce-scatter.11
  1113.8 25.7 reduce-scatter.13
  1142.4 41.1 all-reduce.35
where the time goes:
time: 1230 us; the launch traced here: 1220 us
  waiting for transfers between devices  593 us (48%)
  matrix products  220 us (18%)
  blocking collectives  189 us (15%)
  other arithmetic  164 us (13%)
  local copies, waits for them, and re-layouts  30.3 us (2%)
  between operations  17 us (1%)
    psum x8, waiting for transfers between devices, tensor_total(): lax.psum(partial_value.astype(jnp.bfloat16), 'tp').astype(jnp.float32)  241 us
    psum x1, blocking collectives, per_device(): lax.psum((gain_terms, kernel_local), ('fsdp', 'ctx'))  59.7 us
    convert_element_type x1, other arithmetic, attend_back(): score_grad = (probs * (probs_grad - center)).astype(jnp.bfloat16)  52.7 us
    dot_general x1, matrix products, attend_back(): jnp.einsum('fhe,lhe->hfl', mixed_grad, values, preferred_element_type=jnp...  45.1 us
    psum x1, blocking collectives, per_device(): lax.psum((jnp.sum(shifted_grad, (0, 1)), jnp.sum(shifted_grad * unit, (0,...  33.7 us
    psum x1, blocking collectives, per_device(): lax.psum((jnp.sum(live_cube * filtered, (0, 1)), jnp.sum(live_cube * filt...  32.1 us
    reduce_scatter x1, waiting for transfers between devices, per_device(): lax.psum_scatter(weight_grads[0].astype(jnp.bfloat16), 'fsdp', scatter_di...  29.1 us
    all_gather x1, waiting for transfers between devices, per_device(): lax.all_gather(feed_up, 'fsdp', axis=0, tiled=True)  28.7 us
  transfers between devices with their start and end apart: 27, of which 23 were waited for; matrix products, arithmetic and copies ran while one was open for 6% of the time, Pallas kernels for 0%

commit v1 on v0

--- a/solution.py
+++ b/solution.py
@@ -1,3 +1,4 @@
+import functools
 import jax
 import jax.numpy as jnp
 from jax import lax
@@ -7,6 +8,13 @@
 KERNEL = 31
 norm_eps = 1e-05
 masked_score = -1000000000.0
+
+
+def _expand_meshes(w_in, mesh_name):
+    return lax.all_gather(w_in, axis_name=mesh_name).sum(axis=0)
+
+
+test_vector_on = functools.partial(_expand_meshes, mesh_name="tp")
 
 
 def with_halo(cells, sides, width):
@@ -48,7 +56,7 @@
 
 
 def tensor_total(partial_value):
-    return lax.psum(partial_value.astype(jnp.bfloat16), "tp").astype(jnp.float32)
+    return test_vector_on(partial_value.astype(jnp.bfloat16)).astype(jnp.float32)
 
 
 def product_rows(left, right):

time: 1230 us -> 1170 us (0.951)
  waiting for transfers between devices: 593 us -> 522 us
  other arithmetic: 164 us -> 180 us
    psum x8 -> x0, waiting for transfers between devices: 241 us -> none  [tensor_total(): lax.psum(partial_value.astype(jnp.bfloat16), 'tp').astype(jnp.float32)]
    all_gather x0 -> x8, waiting for transfers between devices: none -> 194 us  [_expand_meshes(): return lax.all_gather(w_in, axis_name=mesh_name).sum(axis=0)]
    reduce_scatter x1, waiting for transfers between devices: 27.7 us -> 4.11 us  [per_device(): lax.psum_scatter(weight_grads[6].astype(jnp.bfloat16), 'fsdp', scatter_di...]
    reduce_sum x0 -> x8, other arithmetic: none -> 20.9 us  [_expand_meshes(): return lax.all_gather(w_in, axis_name=mesh_name).sum(axis=0)]
  transfers between devices with their start and end apart: 27 -> 27, of which waited for: 23 -> 23; matrix products, arithmetic and copies ran while one was open for 6% -> 8% of each run, Pallas kernels for 0% -> 0%
where the time goes in v1:
time: 1170 us; the launch traced here: 1160 us
  waiting for transfers between devices  522 us (45%)
  matrix products  213 us (18%)
  blocking collectives  187 us (16%)
  other arithmetic  180 us (15%)
  local copies, waits for them, and re-layouts  32.7 us (3%)
  between operations  17.8 us (2%)
    all_gather x8, waiting for transfers between devices, _expand_meshes(): return lax.all_gather(w_in, axis_name=mesh_name).sum(axis=0)  194 us
    psum x1, blocking collectives, per_device(): lax.psum((gain_terms, kernel_local), ('fsdp', 'ctx'))  59 us
    convert_element_type x1, other arithmetic, attend_back(): score_grad = (probs * (probs_grad - center)).astype(jnp.bfloat16)  52.7 us
    dot_general x1, matrix products, attend_back(): jnp.einsum('fhe,lhe->hfl', mixed_grad, values, preferred_element_type=jnp...  45 us
    psum x1, blocking collectives, per_device(): lax.psum((jnp.sum(shifted_grad, (0, 1)), jnp.sum(shifted_grad * unit, (0,...  33 us
    psum x1, blocking collectives, per_device(): lax.psum((jnp.sum(live_cube * filtered, (0, 1)), jnp.sum(live_cube * filt...  32 us
    reduce_scatter x1, waiting for transfers between devices, per_device(): lax.psum_scatter(weight_grads[0].astype(jnp.bfloat16), 'fsdp', scatter_di...  29.1 us
    all_gather x1, waiting for transfers between devices, per_device(): lax.all_gather(feed_up, 'fsdp', axis=0, tiled=True)  28.7 us
  transfers between devices with their start and end apart: 27, of which 23 were waited for; matrix products, arithmetic and copies ran while one was open for 8% of the time, Pallas kernels for 0%

profile of v1, /device:TPU:0, one launch (start us, length us, event | category | flops | bytes accessed | tf_op | source)
XLA Modules:
  0.0 1161.4 jit_solution(15022702373127900767)
XLA Ops:
  11.6 28.7 %all-gather.22.cloned.1.call-done = bf16[512,1024]{1,0:T(8,128)(2,1)} async-done(((bf16[128,1024]{1,0:T(8,128)(2,1)}), bf16[512,1024]{1,0:T(8,128)(2,1)}) %all-gather.22.cloned.1.call-update) | async-done | bytes 1048592 | tf_op jit(solution)/shard_map/all_gather | solution.py:165
  40.3 5.1 multiply_convert_fusion.2
  45.4 23.9 %all-gather.24.cloned.1.call-done = bf16[512,1024]{1,0:T(8,128)(2,1)} async-done(((bf16[128,1024]{1,0:T(8,128)(2,1)}), bf16[512,1024]{1,0:T(8,128)(2,1)}) %all-gather.24.cloned.1.call-update) | async-done | bytes 1048592 | tf_op jit(solution)/shard_map/all_gather | solution.py:166
  69.3 4.1 convolution_convert_fusion.10
  73.5 18.0 %all_gather.79 = bf16[512,3,256]{2,0,1:T(8,128)(2,1)S(1)} all-gather(bf16[128,3,256]{2,0,1:T(8,128)(2,1)S(1)} %copy-done.74), channel_id=1, replica_groups=mesh['fsdp'=4,'ctx'=4,'tp'=2] {'fsdp'}, dimensions={0}, use_global_device_ids=true | all-gather | bytes 983040 | tf_op jit(solution)/shard_map/all_gather | solution.py:167
  93.3 12.8 %all-gather.32.cloned.1.call-done = bf16[2048,512]{1,0:T(8,128)(2,1)} async-done(((bf16[1024,512]{1,0:T(8,128)(2,1)}), bf16[2048,512]{1,0:T(8,128)(2,1)}) %all-gather.32.cloned.1.call-update) | async-done | bytes 2097168 | tf_op jit(solution)/shard_map/all_gather | solution.py:14
  106.1 2.6 reduce_sum.727
  114.5 14.0 %all_gather.81 = bf16[512,256]{1,0:T(8,128)(2,1)S(1)} all-gather(bf16[128,256]{1,0:T(8,128)(2,1)S(1)} %copy-done.100), channel_id=1, replica_groups=mesh['fsdp'=4,'ctx'=4,'tp'=2] {'fsdp'}, dimensions={0}, use_global_device_ids=true | all-gather | bytes 327680 | tf_op jit(solution)/shard_map/all_gather | solution.py:168
  128.6 19.9 %all-gather.26.cloned.1.call-done = bf16[1,4096,512]{1,2,0:T(8,128)(2,1)} async-done(((bf16[1,1024,512]{1,2,0:T(8,128)(2,1)}), bf16[1,4096,512]{1,2,0:T(8,128)(2,1)}) %all-gather.26.cloned.1.call-update) | async-done | bytes 4194320 | tf_op jit(solution)/shard_map/all_gather | solution.py:198
  148.4 4.0 fusion.282
  152.4 23.2 %select_reduce_fusion = (f32[4,1024]{1,0:T(4,128)S(1)}, f32[4,1024,4096]{2,1,0:T(8,128)}) fusion(pred[4096]{0:T(1024)(128)(4,1)S(1)} %iota_compare_fusion, bf16[4096,4,64]{0,2,1:T(8,128)(2,1)S(1)} %bitcast.334, f32[1024,4,32]{0,2,1:T(8,128)S(1)} %get-tuple-element.158, f32[1024,4,32]{0,2,1:T(8,128)S(1)} %get-tuple-element.157), kind=kOutput, calls=%fused_computation.6 | convolution fusion | flops 2181820416 | bytes 70275072 | tf_op jit(solution)/shard_map/while/body/eval_jaxpr/fhe,lhe->hfl/dot_general | solution.py:105
  175.6 21.4 %fusion = f32[4,1024]{1,0:T(4,128)S(1)} fusion(f32[4,1024,4096]{2,1,0:T(8,128)} %get-tuple-element.216, f32[4,1024]{1,0:T(4,128)S(1)} %get-tuple-element.215, pred[4096]{0:T(1024)(128)(4,1)S(1)} %iota_compare_fusion), kind=kLoop, calls=%fused_computation.5 | loop fusion | flops 50327552 | bytes 67145728 | tf_op jit(solution)/shard_map/while/body/eval_jaxpr/reduce_sum | solution.py:116
  197.0 23.9 %fusion.55 = bf16[4,64,1024]{2,1,0:T(8,128)(2,1)S(1)} fusion(bf16[4096,4,64]{0,2,1:T(8,128)(2,1)S(1)} %bitcast.340, f32[4,1024,4096]{2,1,0:T(8,128)} %get-tuple-element.216, f32[4,1024]{1,0:T(4,128)S(1)} %fusion, f32[4,1024]{1,0:T(4,128)S(1)} %get-tuple-element.215, pred[4096]{0:T(1024)(128)(4,1)S(1)} %iota_compare_fusion), kind=kOutput, calls=%fused_computation.258 | convolution fusion | flops 2214854656 | bytes 69767168 | tf_op jit(solution)/shard_map/while/body/eval_jaxpr/hfl,lhe->fhe/dot_general | solution.py:118
  222.7 16.5 %all_gather.84 = bf16[512,2,256]{2,0,1:T(8,128)(2,1)} all-gather(bf16[128,2,256]{2,0,1:T(8,128)(2,1)S(1)} %copy.28), channel_id=1, replica_groups=mesh['fsdp'=4,'ctx'=4,'tp'=2] {'fsdp'}, dimensions={0}, use_global_device_ids=true | all-gather | bytes 655360 | tf_op jit(solution)/shard_map/all_gather | solution.py:169
  240.5 15.3 %all-gather.34.cloned.1.call-done = bf16[2048,512]{1,0:T(8,128)(2,1)} async-done(((bf16[1024,512]{1,0:T(8,128)(2,1)}), bf16[2048,512]{1,0:T(8,128)(2,1)}) %all-gather.34.cloned.1.call-update) | async-done | bytes 2097168 | tf_op jit(solution)/shard_map/all_gather | solution.py:14
  255.8 2.6 reduce_sum.731
  265.9 14.7 %all_gather.85 = bf16[512,256]{1,0:T(8,128)(2,1)S(1)} all-gather(bf16[128,256]{1,0:T(8,128)(2,1)S(1)} %copy-done.101), channel_id=1, replica_groups=mesh['fsdp'=4,'ctx'=4,'tp'=2] {'fsdp'}, dimensions={0}, use_global_device_ids=true | all-gather | bytes 327680 | tf_op jit(solution)/shard_map/all_gather | solution.py:170
  281.5 8.0 fusion.86
  289.5 32.0 %all-reduce.8 = (f32[256]{0:T(256)S(1)}, f32[]{:T(128)}, f32[256]{0:T(256)S(1)}) all-reduce(f32[256]{0:T(256)S(1)} %get-tuple-element.109, f32[]{:T(128)} %fusion.247, f32[256]{0:T(256)S(1)} %get-tuple-element.108), channel_id=1, replica_groups=mesh['fsdp'=4,'ctx'=4,'tp'=2] {'fsdp','ctx'}, use_global_device_ids=true, to_apply=%region_11.12 | all-reduce | flops 513 | bytes 4104 | tf_op jit(solution)/shard_map/psum | solution.py:219
  325.8 28.0 %all-gather.36.cloned.1.call-done = bf16[2048,512]{1,0:T(8,128)(2,1)} async-done(((bf16[1024,512]{1,0:T(8,128)(2,1)}), bf16[2048,512]{1,0:T(8,128)(2,1)}) %all-gather.36.cloned.1.call-update) | async-done | bytes 2097168 | tf_op jit(solution)/shard_map/all_gather | solution.py:14
  353.8 2.6 reduce_sum.737
  359.2 24.2 %all-gather.28.cloned.1.call-done = bf16[512,1024]{1,0:T(8,128)(2,1)} async-done(((bf16[128,1024]{1,0:T(8,128)(2,1)}), bf16[512,1024]{1,0:T(8,128)(2,1)}) %all-gather.28.cloned.1.call-update) | async-done | bytes 1048592 | tf_op jit(solution)/shard_map/all_gather | solution.py:171
  383.4 5.0 multiply_convert_fusion.1
  388.5 23.9 %all-gather.30.cloned.1.call-done = bf16[512,1024]{1,0:T(8,128)(2,1)} async-done(((bf16[128,1024]{1,0:T(8,128)(2,1)}), bf16[512,1024]{1,0:T(8,128)(2,1)}) %all-gather.30.cloned.1.call-update) | async-done | bytes 1048592 | tf_op jit(solution)/shard_map/all_gather | solution.py:172
  412.4 4.1 convolution_convert_fusion.7
  417.0 32.2 %all-gather.38.cloned.1.call-done = bf16[2048,512]{1,0:T(8,128)(2,1)} async-done(((bf16[1024,512]{1,0:T(8,128)(2,1)}), bf16[2048,512]{1,0:T(8,128)(2,1)}) %all-gather.38.cloned.1.call-update) | async-done | bytes 2097168 | tf_op jit(solution)/shard_map/all_gather | solution.py:14
  449.1 2.6 reduce_sum.740
  464.7 33.2 %all-gather.40.cloned.1.call-done = bf16[2048,512]{1,0:T(8,128)(2,1)} async-done(((bf16[1024,512]{1,0:T(8,128)(2,1)}), bf16[2048,512]{1,0:T(8,128)(2,1)}) %all-gather.40.cloned.1.call-update) | async-done | bytes 2097168 | tf_op jit(solution)/shard_map/all_gather | solution.py:14
  497.9 2.6 reduce_sum.745
  507.8 33.0 %all-reduce.7 = (f32[256]{0:T(256)S(1)}, f32[256]{0:T(256)S(1)}) all-reduce(f32[256]{0:T(256)S(1)} %get-tuple-element.219, f32[256]{0:T(256)S(1)} %reduce_sum.748), channel_id=1, replica_groups=mesh['fsdp'=4,'ctx'=4,'tp'=2] {'fsdp','ctx'}, use_global_device_ids=true, to_apply=%region_30.31 | all-reduce | flops 512 | bytes 4096 | tf_op jit(solution)/shard_map/psum | solution.py:249
  541.5 5.4 fusion.140
  548.3 3.2 collective-permute-start.3
  552.3 8.5 fusion.89
  564.1 31.1 %all-gather.42.cloned.1.call-done = bf16[2048,512]{1,0:T(8,128)(2,1)} async-done(((bf16[1024,512]{1,0:T(8,128)(2,1)}), bf16[2048,512]{1,0:T(8,128)(2,1)}) %all-gather.42.cloned.1.call-update) | async-done | bytes 2097168 | tf_op jit(solution)/shard_map/all_gather | solution.py:14
  595.2 2.6 reduce_sum.750
  601.6 24.1 %fusion.6 = bf16[4,64,4096]{2,1,0:T(8,128)(2,1)S(1)} fusion(bf16[1024,4,64]{0,2,1:T(8,128)(2,1)S(1)} %bitcast.338, f32[4,1024,4096]{2,1,0:T(8,128)} %get-tuple-element.216, f32[4,1024]{1,0:T(4,128)S(1)} %log_add_fusion, pred[4096]{0:T(1024)(128)(4,1)S(1)} %iota_compare_fusion), kind=kOutput, calls=%fused_computation.45 | convolution fusion | flops 2198863872 | bytes 69750784 | tf_op jit(solution)/shard_map/while/body/eval_jaxpr/hfl,fhe->lhe/dot_general | solution.py:132
  625.7 45.0 %multiply_reduce_fusion = (f32[4,1024]{1,0:T(4,128)S(1)}, f32[4,1024,4096]{2,1,0:T(8,128)}) fusion(f32[4,1024,4096]{2,1,0:T(8,128)} %get-tuple-element.216, f32[4,1024]{1,0:T(4,128)S(1)} %log_add_fusion, pred[4096]{0:T(1024)(128)(4,1)S(1)} %iota_compare_fusion, bf16[1024,4,64]{0,2,1:T(8,128)(2,1)S(1)} %bitcast.339, bf16[4096,4,64]{0,2,1:T(8,128)(2,1)S(1)} %bitcast.341), kind=kOutput, calls=%fused_computation.1 | convolution fusion | flops 2214588416 | bytes 136876032 | tf_op jit(solution)/shard_map/while/body/eval_jaxpr/fhe,lhe->hfl/dot_general | solution.py:127
  673.2 52.7 %multiply_convert_fusion = bf16[4,1024,4096]{2,1,0:T(8,128)(2,1)} fusion(f32[4,1024,4096]{2,1,0:T(8,128)} %get-tuple-element.222, f32[4,1024,4096]{2,1,0:T(8,128)} %get-tuple-element.216, f32[4,1024]{1,0:T(4,128)S(1)} %get-tuple-element.221, f32[4,1024]{1,0:T(4,128)S(1)} %log_add_fusion, pred[4096]{0:T(1024)(128)(4,1)S(1)} %iota_compare_fusion), kind=kLoop, calls=%fused_computation | loop fusion | flops 83886080 | bytes 167809024 | tf_op jit(solution)/shard_map/while/body/eval_jaxpr/convert_element_type | solution.py:129
  726.0 13.8 %convolution_convert_fusion = bf16[4,64,4096]{2,1,0:T(8,128)(2,1)S(1)} fusion(bf16[4,1024,4096]{2,1,0:T(8,128)(2,1)} %multiply_convert_fusion, f32[1024,4,32]{0,2,1:T(8,128)S(1)} %copy-done.45, f32[1024,4,32]{0,2,1:T(8,128)S(1)} %copy-done.43), kind=kOutput, calls=%fused_computation.46 | convolution fusion | flops 2149318656 | bytes 36700160 | tf_op jit(solution)/shard_map/while/body/eval_jaxpr/hfl,fhe->lhe/dot_general | solution.py:131
  742.3 4.5 pad_maximum_fusion
  748.4 17.2 %fusion.54 = f32[1,1024,4,64]{1,3,2,0:T(8,128)S(1)} fusion(bf16[4096,4,64]{0,2,1:T(8,128)(2,1)S(1)} %bitcast.335, bf16[4,1024,4096]{2,1,0:T(8,128)(2,1)} %multiply_convert_fusion), kind=kOutput, calls=%fused_computation.224 | convolution fusion | flops 2147745792 | bytes 36700160 | tf_op jit(solution)/shard_map/while/body/eval_jaxpr/hfl,lhe->fhe/dot_general | solution.py:130
  765.6 25.9 %reduce-scatter.10.cloned.1.call-done = bf16[1,1024,512]{2,1,0:T(8,128)(2,1)} async-done(((bf16[1,4096,512]{2,1,0:T(8,128)(2,1)}), bf16[1,1024,512]{2,1,0:T(8,128)(2,1)}) %reduce-scatter.10.cloned.1.call-update) | async-done | bytes 1048592 | tf_op jit(solution)/shard_map/reduce_scatter | solution.py:291
  797.7 33.2 %all-gather.44.cloned.1.call-done = bf16[2048,512]{1,0:T(8,128)(2,1)} async-done(((bf16[1024,512]{1,0:T(8,128)(2,1)}), bf16[2048,512]{1,0:T(8,128)(2,1)}) %all-gather.44.cloned.1.call-update) | async-done | bytes 2097168 | tf_op jit(solution)/shard_map/all_gather | solution.py:14
  830.9 2.6 reduce_sum.754
  845.1 4.0 convolution_convert_fusion.2
  849.4 5.0 convolution_convert_fusion.1
  854.5 3.2 convolution_convert_fusion.13
  857.8 4.2 convolution_convert_fusion.11
  862.1 4.0 convolution_convert_fusion.4
  866.3 3.9 convolution_convert_fusion.3
  870.2 8.0 all-gather.46.cloned.1.call-done
  878.2 2.6 reduce_sum.757
  882.6 2.7 fusion.50
  885.5 8.6 fusion.36
  895.4 4.2 multiply_multiply_fusion
  903.6 4.1 reduce-scatter.24.cloned.1.call-done
  907.7 28.0 %reduce-scatter.26.cloned.1.call-done = bf16[128,1024]{1,0:T(8,128)(2,1)} async-done(((bf16[512,1024]{1,0:T(8,128)(2,1)}), bf16[128,1024]{1,0:T(8,128)(2,1)}) %reduce-scatter.26.cloned.1.call-update) | async-done | bytes 262160 | tf_op jit(solution)/shard_map/reduce_scatter | solution.py:348
  935.7 23.1 %reduce-scatter.20.cloned.1.call-done = bf16[128,2,256]{2,0,1:T(8,128)(2,1)} async-done(((bf16[512,2,256]{2,0,1:T(8,128)(2,1)}), bf16[128,2,256]{2,0,1:T(8,128)(2,1)}) %reduce-scatter.20.cloned.1.call-update) | async-done | bytes 131088 | tf_op jit(solution)/shard_map/reduce_scatter | solution.py:339
  958.7 23.6 %reduce-scatter.16.cloned.1.call-done = bf16[128,3,256]{2,0,1:T(8,128)(2,1)} async-done(((bf16[512,3,256]{2,0,1:T(8,128)(2,1)}), bf16[128,3,256]{2,0,1:T(8,128)(2,1)}) %reduce-scatter.16.cloned.1.call-update) | async-done | bytes 196624 | tf_op jit(solution)/shard_map/reduce_scatter | solution.py:333
  982.3 29.1 %reduce-scatter.12.cloned.1.call-done = bf16[128,1024]{1,0:T(8,128)(2,1)} async-done(((bf16[512,1024]{1,0:T(8,128)(2,1)}), bf16[128,1024]{1,0:T(8,128)(2,1)}) %reduce-scatter.12.cloned.1.call-update) | async-done | bytes 262160 | tf_op jit(solution)/shard_map/reduce_scatter | solution.py:327
  1011.4 27.9 %reduce-scatter.14.cloned.1.call-done = bf16[128,1024]{1,0:T(8,128)(2,1)} async-done(((bf16[512,1024]{1,0:T(8,128)(2,1)}), bf16[128,1024]{1,0:T(8,128)(2,1)}) %reduce-scatter.14.cloned.1.call-update) | async-done | bytes 262160 | tf_op jit(solution)/shard_map/reduce_scatter | solution.py:330
  1039.4 21.3 %reduce-scatter.18.cloned.1.call-done = bf16[128,256]{1,0:T(8,128)(2,1)} async-done(((bf16[512,256]{1,0:T(8,128)(2,1)}), bf16[128,256]{1,0:T(8,128)(2,1)}) %reduce-scatter.18.cloned.1.call-update) | async-done | bytes 65552 | tf_op jit(solution)/shard_map/reduce_scatter | solution.py:336
  1060.7 21.1 %reduce-scatter.22.cloned.1.call-done = bf16[128,256]{1,0:T(8,128)(2,1)} async-done(((bf16[512,256]{1,0:T(8,128)(2,1)}), bf16[128,256]{1,0:T(8,128)(2,1)}) %reduce-scatter.22.cloned.1.call-update) | async-done | bytes 65552 | tf_op jit(solution)/shard_map/reduce_scatter | solution.py:342
  1084.8 59.0 %all-reduce.6 = (f32[5,512]{1,0:T(8,128)}, f32[31,256]{1,0:T(8,128)}) all-reduce(f32[5,512]{1,0:T(8,128)S(1)} %stack.128, f32[31,256]{1,0:T(8,128)S(1)} %stack.160), channel_id=1, replica_groups=mesh['fsdp'=4,'ctx'=4,'tp'=2] {'fsdp','ctx'}, use_global_device_ids=true, to_apply=%region_47.48 | all-reduce | flops 10496 | bytes 83968 | tf_op jit(solution)/shard_map/psum | solution.py:315
  (557 shorter events, 103.6 us)
Async XLA Ops:
  7.2 33.1 %all-gather.22.cloned.1.call-start = ((), (), s32[]{:S(2)}) async-start(), calls=%async_computation.9 | async-start | bytes 1310720 | tf_op jit(solution)/shard_map/all_gather | solution.py:165
  7.9 61.3 %all-gather.24.cloned.1.call-start = ((), (), s32[]{:S(2)}) async-start(), calls=%async_computation.10 | async-start | bytes 1310720 | tf_op jit(solution)/shard_map/all_gather | solution.py:166
  8.7 97.4 %all-gather.32.cloned.1.call-start = ((), (), s32[]{:S(2)}) async-start(), calls=%async_computation.23 | async-start | bytes 3145728 | tf_op jit(solution)/shard_map/all_gather | solution.py:14
  11.6 97.9 %copy-start.104 = (f32[1,512]{1,0:T(1,128)}, f32[1,512]{1,0:T(1,128)S(1)}, u32[]{:S(2)}) copy-start(f32[1,512]{1,0:T(1,128)S(1)} %get-tuple-element.204) | copy-start | bytes 6148
  11.6 587.6 %copy-start.102 = (f32[1,512]{1,0:T(1,128)}, f32[1,512]{1,0:T(1,128)S(1)}, u32[]{:S(2)}) copy-start(f32[1,512]{1,0:T(1,128)S(1)} %get-tuple-element.203) | copy-start | bytes 6148
  73.4 75.0 %all-gather.26.cloned.1.call-start = ((), (), s32[]{:S(2)}) async-start(), calls=%async_computation.11 | async-start | bytes 5242880 | tf_op jit(solution)/shard_map/all_gather | solution.py:198
  113.8 142.0 %all-gather.34.cloned.1.call-start = ((), (), s32[]{:S(2)}) async-start(), calls=%async_computation.24 | async-start | bytes 3145728 | tf_op jit(solution)/shard_map/all_gather | solution.py:14
  222.6 131.3 %all-gather.36.cloned.1.call-start = ((), (), s32[]{:S(2)}) async-start(), calls=%async_computation.25 | async-start | bytes 3145728 | tf_op jit(solution)/shard_map/all_gather | solution.py:14
  239.8 301.1 %copy-start.127 = (f32[1,256]{1,0:T(1,128)}, f32[1,256]{1,0:T(1,128)S(1)}, u32[]{:S(2)}) copy-start(f32[1,256]{1,0:T(1,128)S(1)} %get-tuple-element.211) | copy-start | bytes 3076
  259.4 339.8 %copy-start.81 = (f32[1024]{0:T(1024)}, f32[1024]{0:T(1024)S(1)}, u32[]{:S(2)}) copy-start(f32[1024]{0:T(1024)S(1)} %broadcast_multiply_fusion.2) | copy-start | bytes 12292
  259.9 339.4 %copy-start.92 = (f32[1024]{0:T(1024)}, f32[1024]{0:T(1024)S(1)}, u32[]{:S(2)}) copy-start(f32[1024]{0:T(1024)S(1)} %fusion.244) | copy-start | bytes 12292
  261.8 60.9 %copy-start.189 = (f32[1,256]{1,0:T(1,128)S(1)}, f32[1,256]{1,0:T(1,128)}, u32[]{:S(2)}) copy-start(f32[1,256]{1,0:T(1,128)} %get-tuple-element.212) | copy-start | bytes 3076
  263.0 18.2 %collective-permute-start = (bf16[1,15,256]{2,1,0:T(8,128)(2,1)S(1)}, bf16[1,15,256]{2,1,0:T(8,128)(2,1)S(1)}, u32[]{:S(2)}, u32[]{:S(2)}) collective-permute-start(bf16[1,15,256]{2,1,0:T(8,128)(2,1)S(1)} %get-tuple-element.165), channel_id=1, source_target_pairs={{0,2},{2,4},{4,6},{1,3},{3,5},{5,7},{8,10},{10,12},{12,14},{9,11},... | collective-permute-start | bytes 23048 | tf_op jit(solution)/shard_map/ppermute | solution.py:28
  264.6 16.7 %collective-permute-start.1 = (bf16[1,15,256]{2,1,0:T(8,128)(2,1)S(1)}, bf16[1,15,256]{2,1,0:T(8,128)(2,1)S(1)}, u32[]{:S(2)}, u32[]{:S(2)}) collective-permute-start(bf16[1,15,256]{2,1,0:T(8,128)(2,1)S(1)} %get-tuple-element.166), channel_id=1, source_target_pairs={{2,0},{4,2},{6,4},{3,1},{5,3},{7,5},{10,8},{12,10},{14,12},{11,9},... | collective-permute-start | bytes 23048 | tf_op jit(solution)/shard_map/ppermute | solution.py:30
  281.3 260.3 %copy-start.83 = (bf16[1,15,256]{2,1,0:T(8,128)(2,1)}, bf16[1,15,256]{2,1,0:T(8,128)(2,1)S(1)}, u32[]{:S(2)}) copy-start(bf16[1,15,256]{2,1,0:T(8,128)(2,1)S(1)} %collective-permute-done.1) | copy-start | bytes 23044
  324.3 59.1 %all-gather.28.cloned.1.call-start = ((), (), s32[]{:S(2)}) async-start(), calls=%async_computation.12 | async-start | bytes 1310720 | tf_op jit(solution)/shard_map/all_gather | solution.py:171
  325.0 87.4 %all-gather.30.cloned.1.call-start = ((), (), s32[]{:S(2)}) async-start(), calls=%async_computation.13 | async-start | bytes 1310720 | tf_op jit(solution)/shard_map/all_gather | solution.py:172
  325.8 123.4 %all-gather.38.cloned.1.call-start = ((), (), s32[]{:S(2)}) async-start(), calls=%async_computation.26 | async-start | bytes 3145728 | tf_op jit(solution)/shard_map/all_gather | solution.py:14
  358.7 144.3 %copy-start = (f32[1024,512]{1,0:T(8,128)}, f32[1024,512]{1,0:T(8,128)S(1)}, u32[]{:S(2)}) copy-start(f32[1024,512]{1,0:T(8,128)S(1)} %get-tuple-element.143) | copy-start | bytes 6291460
  358.8 144.3 %copy-start.79 = (f32[1024]{0:T(1024)}, f32[1024]{0:T(1024)S(1)}, u32[]{:S(2)}) copy-start(f32[1024]{0:T(1024)S(1)} %broadcast_multiply_fusion.1) | copy-start | bytes 12292
  359.2 143.8 %copy-start.98 = (f32[1024]{0:T(1024)}, f32[1024]{0:T(1024)S(1)}, u32[]{:S(2)}) copy-start(f32[1024]{0:T(1024)S(1)} %fusion.245) | copy-start | bytes 12292
  416.5 81.4 %all-gather.40.cloned.1.call-start = ((), (), s32[]{:S(2)}) async-start(), calls=%async_computation.27 | async-start | bytes 3145728 | tf_op jit(solution)/shard_map/all_gather | solution.py:14
  456.5 46.5 %copy-start.116 = (f32[1024]{0:T(1024)}, f32[1024]{0:T(1024)S(1)}, u32[]{:S(2)}) copy-start(f32[1024]{0:T(1024)S(1)} %negate_multiply_fusion.4) | copy-start | bytes 12292
  464.6 130.6 %all-gather.42.cloned.1.call-start = ((), (), s32[]{:S(2)}) async-start(), calls=%async_computation.28 | async-start | bytes 3145728 | tf_op jit(solution)/shard_map/all_gather | solution.py:14
  506.2 46.0 %copy-start.22 = (f32[1024,2,256]{2,0,1:T(8,128)S(1)}, f32[1024,2,256]{2,0,1:T(8,128)}, u32[]{:S(2)}) copy-start(f32[1024,2,256]{2,0,1:T(8,128)} %copy-done.21) | copy-start | bytes 6291460
  506.2 46.0 %copy-start.130 = (f32[1,256]{1,0:T(1,128)S(1)}, f32[1,256]{1,0:T(1,128)}, u32[]{:S(2)}) copy-start(f32[1,256]{1,0:T(1,128)} %copy-done.129) | copy-start | bytes 3076
  506.2 46.0 %copy-start.132 = (f32[1,256]{1,0:T(1,128)S(1)}, f32[1,256]{1,0:T(1,128)}, u32[]{:S(2)}) copy-start(f32[1,256]{1,0:T(1,128)} %copy-done.131) | copy-start | bytes 3076
  506.2 46.0 %copy-start.134 = (f32[1,256]{1,0:T(1,128)S(1)}, f32[1,256]{1,0:T(1,128)}, u32[]{:S(2)}) copy-start(f32[1,256]{1,0:T(1,128)} %copy-done.133) | copy-start | bytes 3076
  506.2 46.0 %copy-start.136 = (f32[1,256]{1,0:T(1,128)S(1)}, f32[1,256]{1,0:T(1,128)}, u32[]{:S(2)}) copy-start(f32[1,256]{1,0:T(1,128)} %copy-done.135) | copy-start | bytes 3076
  506.2 46.0 %copy-start.138 = (f32[1,256]{1,0:T(1,128)S(1)}, f32[1,256]{1,0:T(1,128)}, u32[]{:S(2)}) copy-start(f32[1,256]{1,0:T(1,128)} %get-tuple-element.176) | copy-start | bytes 3076
  506.2 46.0 %copy-start.140 = (f32[1,256]{1,0:T(1,128)S(1)}, f32[1,256]{1,0:T(1,128)}, u32[]{:S(2)}) copy-start(f32[1,256]{1,0:T(1,128)} %get-tuple-element.177) | copy-start | bytes 3076
  506.2 46.0 %copy-start.142 = (f32[1,256]{1,0:T(1,128)S(1)}, f32[1,256]{1,0:T(1,128)}, u32[]{:S(2)}) copy-start(f32[1,256]{1,0:T(1,128)} %get-tuple-element.178) | copy-start | bytes 3076
  506.2 46.0 %copy-start.144 = (f32[1,256]{1,0:T(1,128)S(1)}, f32[1,256]{1,0:T(1,128)}, u32[]{:S(2)}) copy-start(f32[1,256]{1,0:T(1,128)} %get-tuple-element.179) | copy-start | bytes 3076
  506.2 46.0 %copy-start.146 = (f32[1,256]{1,0:T(1,128)S(1)}, f32[1,256]{1,0:T(1,128)}, u32[]{:S(2)}) copy-start(f32[1,256]{1,0:T(1,128)} %get-tuple-element.180) | copy-start | bytes 3076
  506.3 46.0 %copy-start.148 = (f32[1,256]{1,0:T(1,128)S(1)}, f32[1,256]{1,0:T(1,128)}, u32[]{:S(2)}) copy-start(f32[1,256]{1,0:T(1,128)} %get-tuple-element.181) | copy-start | bytes 3076
  506.3 46.0 %copy-start.150 = (f32[1,256]{1,0:T(1,128)S(1)}, f32[1,256]{1,0:T(1,128)}, u32[]{:S(2)}) copy-start(f32[1,256]{1,0:T(1,128)} %get-tuple-element.182) | copy-start | bytes 3076
  506.3 46.0 %copy-start.152 = (f32[1,256]{1,0:T(1,128)S(1)}, f32[1,256]{1,0:T(1,128)}, u32[]{:S(2)}) copy-start(f32[1,256]{1,0:T(1,128)} %get-tuple-element.183) | copy-start | bytes 3076
  547.0 4.5 collective-permute-start.2
  548.3 3.8 collective-permute-start.3
  564.1 227.5 %reduce-scatter.10.cloned.1.call-start = ((), (), s32[]{:S(2)}) async-start(), calls=%async_computation.14 | async-start | bytes 5242880 | tf_op jit(solution)/shard_map/reduce_scatter | solution.py:291
  673.2 52.7 %copy-start.43 = (f32[1024,4,32]{0,2,1:T(8,128)S(1)}, f32[1024,4,32]{0,2,1:T(8,128)}, u32[]{:S(2)}) copy-start(f32[1024,4,32]{0,2,1:T(8,128)} %copy-done.42) | copy-start | bytes 1572868
  673.2 52.7 %copy-start.45 = (f32[1024,4,32]{0,2,1:T(8,128)S(1)}, f32[1024,4,32]{0,2,1:T(8,128)}, u32[]{:S(2)}) copy-start(f32[1024,4,32]{0,2,1:T(8,128)} %copy-done.44) | copy-start | bytes 1572868
  746.8 84.1 %all-gather.44.cloned.1.call-start = ((), (), s32[]{:S(2)}) async-start(), calls=%async_computation.29 | async-start | bytes 3145728 | tf_op jit(solution)/shard_map/all_gather | solution.py:14
  797.7 80.5 %all-gather.46.cloned.1.call-start = ((), (), s32[]{:S(2)}) async-start(), calls=%async_computation.30 | async-start | bytes 3145728 | tf_op jit(solution)/shard_map/all_gather | solution.py:14
  845.0 62.7 %reduce-scatter.24.cloned.1.call-start = ((), (), s32[]{:S(2)}) async-start(), calls=%async_computation.21 | async-start | bytes 1310720 | tf_op jit(solution)/shard_map/reduce_scatter | solution.py:345
  849.1 86.5 %reduce-scatter.26.cloned.1.call-start = ((), (), s32[]{:S(2)}) async-start(), calls=%async_computation.22 | async-start | bytes 1310720 | tf_op jit(solution)/shard_map/reduce_scatter | solution.py:348
  854.4 104.3 %reduce-scatter.20.cloned.1.call-start = ((), (), s32[]{:S(2)}) async-start(), calls=%async_computation.19 | async-start | bytes 655360 | tf_op jit(solution)/shard_map/reduce_scatter | solution.py:339
  857.7 124.6 %reduce-scatter.16.cloned.1.call-start = ((), (), s32[]{:S(2)}) async-start(), calls=%async_computation.17 | async-start | bytes 983040 | tf_op jit(solution)/shard_map/reduce_scatter | solution.py:333
  862.0 149.4 %reduce-scatter.12.cloned.1.call-start = ((), (), s32[]{:S(2)}) async-start(), calls=%async_computation.15 | async-start | bytes 1310720 | tf_op jit(solution)/shard_map/reduce_scatter | solution.py:327
  866.2 173.2 %reduce-scatter.14.cloned.1.call-start = ((), (), s32[]{:S(2)}) async-start(), calls=%async_computation.16 | async-start | bytes 1310720 | tf_op jit(solution)/shard_map/reduce_scatter | solution.py:330
  870.2 190.6 %reduce-scatter.18.cloned.1.call-start = ((), (), s32[]{:S(2)}) async-start(), calls=%async_computation.18 | async-start | bytes 327680 | tf_op jit(solution)/shard_map/reduce_scatter | solution.py:336
  895.3 186.5 %reduce-scatter.22.cloned.1.call-start = ((), (), s32[]{:S(2)}) async-start(), calls=%async_computation.20 | async-start | bytes 327680 | tf_op jit(solution)/shard_map/reduce_scatter | solution.py:342
  901.1 242.7 %all-reduce.12.cloned.1.call-start = ((), (), s32[]{:S(2)}) async-start(), calls=%async_computation.31 | async-start | bytes 3014656 | tf_op jit(solution)/shard_map/psum | solution.py:357
  903.5 180.6 %copy-start.169 = (f32[256]{0:T(256)S(1)}, f32[256]{0:T(256)}, u32[]{:S(2)}) copy-start(f32[256]{0:T(256)} %get-tuple-element.84) | copy-start | bytes 3076
  903.5 180.6 %copy-start.170 = (f32[256]{0:T(256)S(1)}, f32[256]{0:T(256)}, u32[]{:S(2)}) copy-start(f32[256]{0:T(256)} %get-tuple-element.85) | copy-start | bytes 3076
  903.5 180.6 %copy-start.171 = (f32[256]{0:T(256)S(1)}, f32[256]{0:T(256)}, u32[]{:S(2)}) copy-start(f32[256]{0:T(256)} %get-tuple-element.86) | copy-start | bytes 3076
  903.5 180.6 %copy-start.172 = (f32[256]{0:T(256)S(1)}, f32[256]{0:T(256)}, u32[]{:S(2)}) copy-start(f32[256]{0:T(256)} %get-tuple-element.87) | copy-start | bytes 3076
  903.5 180.6 %copy-start.173 = (f32[256]{0:T(256)S(1)}, f32[256]{0:T(256)}, u32[]{:S(2)}) copy-start(f32[256]{0:T(256)} %get-tuple-element.88) | copy-start | bytes 3076
  903.5 180.6 %copy-start.174 = (f32[256]{0:T(256)S(1)}, f32[256]{0:T(256)}, u32[]{:S(2)}) copy-start(f32[256]{0:T(256)} %get-tuple-element.89) | copy-start | bytes 3076
  903.5 180.7 %copy-start.177 = (f32[256]{0:T(256)S(1)}, f32[256]{0:T(256)}, u32[]{:S(2)}) copy-start(f32[256]{0:T(256)} %copy-done.176) | copy-start | bytes 3076
  903.5 180.7 %copy-start.179 = (f32[256]{0:T(256)S(1)}, f32[256]{0:T(256)}, u32[]{:S(2)}) copy-start(f32[256]{0:T(256)} %copy-done.178) | copy-start | bytes 3076
  903.6 181.2 %copy-start.165 = (f32[512]{0:T(512)S(1)}, f32[512]{0:T(512)}, u32[]{:S(2)}) copy-start(f32[512]{0:T(512)} %get-tuple-element.68) | copy-start | bytes 6148
  903.6 181.2 %copy-start.166 = (f32[512]{0:T(512)S(1)}, f32[512]{0:T(512)}, u32[]{:S(2)}) copy-start(f32[512]{0:T(512)} %get-tuple-element.70) | copy-start | bytes 6148
  903.6 181.2 %copy-start.167 = (f32[512]{0:T(512)S(1)}, f32[512]{0:T(512)}, u32[]{:S(2)}) copy-start(f32[512]{0:T(512)} %get-tuple-element.76) | copy-start | bytes 6148
  (163 other events, 1990.9 us)
Sparse Core Ops, SparseCore 0:
  9.6 30.6 all-gather.21
  41.9 27.3 all-gather.23
  73.6 32.4 all-gather.31
  113.9 34.4 all-gather.25
  222.7 33.0 all-gather.33
  324.4 29.4 all-gather.35
  355.4 27.9 all-gather.27
  385.0 27.3 all-gather.29
  416.6 32.4 all-gather.37
  464.7 33.0 all-gather.39
  564.2 30.9 all-gather.41
  746.9 44.5 reduce-scatter.9
  797.8 33.0 all-gather.43
  845.1 33.0 all-gather.45
  880.4 27.2 reduce-scatter.23
  909.8 25.7 reduce-scatter.25
  938.4 20.3 reduce-scatter.19
  960.9 21.3 reduce-scatter.15
  984.6 26.7 reduce-scatter.11
  1013.6 25.7 reduce-scatter.13
  1042.2 18.4 reduce-scatter.17
  1063.6 18.2 reduce-scatter.21
  1084.7 40.9 all-reduce.11
